TPU v7x, 256 devices: a whole 4x4x8 slice. The times are simulated.
256 devices in a mesh: seq: 32 (over y, x, core), tp: 8 (over z).
Axes of the slice: x: 4, y: 4, z: 8, core: 2. Of those that a mesh axis runs over, the one named last changes fastest.
Arguments:
- hidden_in: bfloat16 [2, 16384, 2560], P(None, 'seq'), may hold values from -6 to 6
- gate_proj: bfloat16 [2560, 5120], P(None, 'tp'), may hold values from -0.125 to 0.125
- value_proj: bfloat16 [2560, 5120], P(None, 'tp'), may hold values from -0.125 to 0.125
- bc_proj: bfloat16 [2560, 256], P(None, 'tp'), may hold values from -0.125 to 0.125
- step_proj: bfloat16 [2560, 80], P(None, 'tp'), may hold values from -0.125 to 0.125
- value_conv: float32 [4, 5120], P(None, 'tp'), may hold values from -3 to 3
- bc_conv: float32 [4, 256], replicated, may hold values from -3 to 3
- step_bias: float32 [80], P('tp'), may hold values from -1.5 to 0
- log_rate: float32 [80], P('tp'), as said below
- norm_gain: float32 [5120], P('tp'), may hold values from 0.25 to 1.75
Outputs:
- mixer_out: bfloat16 [2, 16384, 5120], P(None, 'seq', 'tp')
Inputs may be any that keep to these rules, and one draw needn't show every extreme that they name: log_rate lies between -1.5 - ln(16384) and 1.0 - ln(16384).
All inputs are finite; a program needn't handle non-finite values.
Results may differ from a plain program's by a relative error of at most 0.0095.
Values may be sent and summed in bfloat16 or wider, within the bound.
A program may use at most 128 MiB of HBM per device.

v0:
```python
import jax
import jax.numpy as jnp
from jax import lax
from jax.experimental import pallas as pl
from jax.experimental.pallas import tpu as pltpu
from jax.sharding import PartitionSpec as P

DI = 5120
HEAD_DIM = 64
STATE = 128
CONV = 4
BLOCK = 64
PAD = 16
FIRST = PAD - CONV + 1
MESH = pl.DeviceIdType.MESH

epsilon = 1e-05
F32 = jnp.float32
BF16 = jnp.bfloat16


def shifted(block, axis, distance):
    count = lax.axis_size(axis)
    route = [(i, i + distance) for i in range(count - distance)]
    return lax.ppermute(block, axis, route)


def silu(x):
    return x * (1.0 / (1.0 + jnp.exp(-x)))


def spread(x, expand):
    high = x.astype(BF16)
    low = (x - high.astype(F32)).astype(BF16)
    return jnp.dot(jnp.concatenate([high, low], axis=1), expand, preferred_element_type=F32)


def tile_of(width):
    return 256 if width % 256 == 0 else 128


def state_kernel(
    pre_ref, bc_ref, step_ref, kernel_ref, bc_kernel_ref,
    bias_ref, rate_ref, expand_ref,
    scaled_ref, bc_out_ref, fout_ref, em_ref, state_out_ref, decay_ref,
    window, bc_window, lows, state_ref,
):
    length, width = step_ref.shape[1], pre_ref.shape[2]
    tile = tile_of(width)
    window[0:PAD, :] = pre_ref[0, 0:PAD, :].astype(F32)
    bc_window[0:PAD, :] = bc_ref[0, 0:PAD, :].astype(F32)
    state_ref[...] = jnp.zeros_like(state_ref)
    heads = bias_ref.shape[1]
    rows = lax.broadcasted_iota(jnp.int32, (BLOCK, BLOCK), 0)
    cols = lax.broadcasted_iota(jnp.int32, (BLOCK, BLOCK), 1)
    triangle = jnp.where(rows >= cols, 1.0, 0.0).astype(F32)
    lows[...] = jnp.zeros_like(lows)

    @pl.loop(0, length // BLOCK, unroll=4)
    def _(index):
        at = pl.ds(pl.multiple_of(index * BLOCK, BLOCK), BLOCK)
        past = pl.ds(pl.multiple_of(index * BLOCK + PAD, PAD), BLOCK)
        step_pre = step_ref[0, at, :] + bias_ref[...]
        steps = jnp.maximum(step_pre, 0.0) + jnp.log1p(jnp.exp(-jnp.abs(step_pre)))
        log_decay = -steps * jnp.exp(rate_ref[...])
        cumulative = jnp.dot(
            triangle, log_decay, precision=lax.Precision.HIGHEST, preferred_element_type=F32
        )
        last = cumulative[BLOCK - 1 : BLOCK, :]
        lows[0:1, :] += last
        mid = 0.5 * last
        fin = jnp.exp(mid - cumulative) * steps
        fout_ref[0, at, :] = jnp.exp(cumulative - mid)
        em = jnp.broadcast_to(jnp.exp(mid), (8, heads))
        em_ref[0, pl.ds(pl.multiple_of(index * 8, 8), 8), :] = em
        wide_fin = spread(fin, expand_ref[...])
        wide_em = spread(em, expand_ref[...])[0:1, :]

        bc_window[PAD:, :] = bc_ref[0, past, :].astype(F32)
        bc = bc_kernel_ref[0:1, :] * bc_window[FIRST : FIRST + BLOCK, :]
        for k in range(1, CONV):
            bc = bc + bc_kernel_ref[k : k + 1, :] * bc_window[FIRST + k : FIRST + k + BLOCK, :]
        bc = silu(bc).astype(BF16)
        bc_out_ref[0, at, :] = bc
        bc_window[0:PAD, :] = bc_window[BLOCK : BLOCK + PAD, :]
        b_rows = bc[:, :STATE]

        for start in range(0, width, tile):
            cut = slice(start, start + tile)
            window[PAD:, cut] = pre_ref[0, past, cut].astype(F32)
            x = kernel_ref[0:1, cut] * window[FIRST : FIRST + BLOCK, cut]
            for k in range(1, CONV):
                x = x + kernel_ref[k : k + 1, cut] * window[FIRST + k : FIRST + k + BLOCK, cut]
            scaled = (silu(x) * wide_fin[:, cut]).astype(BF16)
            window[0:PAD, cut] = window[BLOCK : BLOCK + PAD, cut]
            scaled_ref[0, at, cut] = scaled
            added = lax.dot_general(
                b_rows, scaled, (((0,), (0,)), ((), ())), preferred_element_type=F32
            )
            e = wide_em[:, cut]
            state_ref[:, cut] = e * (e * state_ref[:, cut] + added)

    state_out_ref[0] = state_ref[...].astype(BF16)
    decay_ref[0] = spread(jnp.exp(lows[...]), expand_ref[...])


def value_kernel(
    hidden_ref, halo_ref, bc_ref, weight_ref,
    pre_ref, bc_out_ref,
    rows, slots, load_sem, send_sem, recv_sem,
):
    batch = hidden_ref.shape[0]
    count = slots.shape[0]
    narrow = bc_ref.shape[1]
    me = lax.axis_index("tp")
    step = pl.program_id(0)

    def sends():
        for away in range(1, count):
            peer = lax.rem(me + away, count)
            yield pltpu.make_async_remote_copy(
                src_ref=bc_ref, dst_ref=slots.at[me],
                send_sem=send_sem.at[away - 1], recv_sem=recv_sem.at[away - 1],
                device_id={"tp": peer}, device_id_type=MESH,
            )

    @pl.when(step == 0)
    def _():
        loads = []
        for b in range(batch):
            loads.append(pltpu.make_async_copy(
                hidden_ref.at[b], rows.at[b, pl.ds(PAD, hidden_ref.shape[1])], load_sem.at[2 * b]
            ))
            loads.append(pltpu.make_async_copy(
                halo_ref.at[b], rows.at[b, pl.ds(0, PAD)], load_sem.at[2 * b + 1]
            ))
        loads.append(pltpu.make_async_copy(bc_ref, slots.at[me], load_sem.at[2 * batch]))
        for load in loads:
            load.start()
        barrier = pltpu.get_barrier_semaphore()
        for away in range(1, count):
            pl.semaphore_signal(
                barrier, inc=1, device_id={"tp": lax.rem(me + away, count)}, device_id_type=MESH
            )
        pl.semaphore_wait(barrier, count - 1)
        for send in sends():
            send.start()
        for load in loads:
            load.wait()

    @pl.loop(0, batch)
    def _(b):
        pre_ref[b] = jnp.dot(
            rows[b], weight_ref[...], preferred_element_type=F32
        ).astype(BF16)

    @pl.when(step == pl.num_programs(0) - 1)
    def _():
        for send in sends():
            send.wait()
        bc_out_ref[...] = jnp.concatenate([slots[k] for k in range(count)], axis=1)


def gate_kernel(
    hidden_ref, weight_ref, local_ref, span_ref,
    gate_ref, before_ref,
    pair, pair_span, sent, sent_span, got, got_span, entering, entering_half, reach,
    send_sem, recv_sem,
):
    step = pl.program_id(0)
    place = lax.axis_index("seq")
    chips = lax.axis_size("seq") // 2
    core = lax.rem(place, 2)
    chip = place // 2
    partner = place + 1 - 2 * core
    half = STATE // 2
    batch = local_ref.shape[0]
    mine = pl.ds(pl.multiple_of(core * half, half), half)
    distances = []
    while 2 ** len(distances) < chips:
        distances.append(2 ** len(distances))

    def copies(source, target, slot, device):
        return pltpu.make_async_remote_copy(
            src_ref=source, dst_ref=target, send_sem=send_sem.at[slot],
            recv_sem=recv_sem.at[slot], device_id={"seq": device}, device_id_type=MESH,
        )

    def pair_copies():
        return (copies(local_ref, pair, 0, partner), copies(span_ref, pair_span, 1, partner))

    def round_copies(r):
        device = lax.rem(place + 2 * distances[r], 2 * chips)
        return (
            copies(sent.at[r], got.at[r], 2 + 2 * r, device),
            copies(sent_span.at[r], got_span.at[r], 3 + 2 * r, device),
        )

    @pl.when(step == 0)
    def _():
        barrier = pltpu.get_barrier_semaphore()
        pl.semaphore_signal(barrier, inc=1, device_id={"seq": partner}, device_id_type=MESH)
        for d in distances:
            for away in (2 * d, 2 * (chips - d)):
                pl.semaphore_signal(
                    barrier, inc=1, device_id={"seq": lax.rem(place + away, 2 * chips)},
                    device_id_type=MESH,
                )
        pl.semaphore_wait(barrier, 1 + 2 * len(distances))
        for copy in pair_copies():
            copy.start()

    def start_round(r):
        @pl.when(chip + distances[r] < chips)
        def _():
            for copy in round_copies(r):
                copy.start()

    @pl.when(step == 1)
    def _():
        for copy in pair_copies():
            copy.wait()
        sent_span[0] = span_ref[...] * pair_span[...]
        reach[...] = jnp.ones_like(reach)
        for b in range(batch):
            own = local_ref[b, mine, :].astype(F32)
            other = pair[b, mine, :].astype(F32)
            first = jnp.where(core == 0, own, other)
            second = jnp.where(core == 0, other, own)
            later = jnp.where(core == 0, pair_span[b : b + 1, :], span_ref[b : b + 1, :])
            sent[0, b] = (later * first + second).astype(BF16)
            entering_half[b] = jnp.zeros((half, own.shape[1]), BF16)
        start_round(0)

    gate_ref[...] = jnp.dot(
        hidden_ref[...], weight_ref[...], preferred_element_type=F32
    ).astype(BF16)

    @pl.when(step == pl.num_programs(0) - 1)
    def _():
        for r, d in enumerate(distances):
            @pl.when(chip + d < chips)
            def _():
                for copy in round_copies(r):
                    copy.wait_send()

            more = r + 1 < len(distances)

            @pl.when(chip >= d)
            def _():
                for copy in round_copies(r):
                    copy.wait_recv()
                for b in range(batch):
                    arrived = got[r, b].astype(F32)
                    entering_half[b] = (
                        entering_half[b].astype(F32) + reach[b : b + 1, :] * arrived
                    ).astype(BF16)
                    if more:
                        sent[r + 1, b] = (
                            sent[r, b].astype(F32) + sent_span[r, b : b + 1, :] * arrived
                        ).astype(BF16)
                reach[...] = reach[...] * got_span[r]
                if more:
                    sent_span[r + 1] = sent_span[r] * got_span[r]

            if more:
                @pl.when(chip < d)
                def _():
                    sent[r + 1] = sent[r]
                    sent_span[r + 1] = sent_span[r]

                start_round(r + 1)
        last = 2 + 2 * len(distances)
        swap = copies(entering_half, entering.at[:, mine, :], last, partner)
        swap.start()
        swap.wait()
        for b in range(batch):
            entering[b, mine, :] = entering_half[b]
        for b in range(batch):
            full = entering[b].astype(F32)
            moved = pair_span[b : b + 1, :] * full + pair[b].astype(F32)
            before_ref[b] = jnp.where(core == 0, full, moved)


def output_kernel(
    scaled_ref, bc_ref, fout_ref, em_ref, state_ref, gate_ref, expand_ref, gain_ref,
    out_ref,
    held, right, gated_all, sums, others, send_sem, recv_sem,
):
    length, width = scaled_ref.shape[1], scaled_ref.shape[2]
    blocks = length // BLOCK
    tile = tile_of(width)
    step = pl.program_id(0)
    batch = pl.num_programs(0) // 2
    rows = lax.broadcasted_iota(jnp.int32, (BLOCK, BLOCK), 0)
    cols = lax.broadcasted_iota(jnp.int32, (BLOCK, BLOCK), 1)
    lane = lax.broadcasted_iota(jnp.int32, (BLOCK, 128), 1)
    count = others.shape[0] + 1
    me = lax.axis_index("tp")

    def sends():
        for away in range(1, count):
            yield pltpu.make_async_remote_copy(
                src_ref=sums, dst_ref=others.at[away - 1],
                send_sem=send_sem.at[away - 1], recv_sem=recv_sem.at[away - 1],
                device_id={"tp": lax.rem(me + away, count)}, device_id_type=MESH,
            )

    @pl.when(step == 0)
    def _():
        sums[...] = jnp.zeros_like(sums)
        barrier = pltpu.get_barrier_semaphore()
        for away in range(1, count):
            pl.semaphore_signal(
                barrier, inc=1, device_id={"tp": lax.rem(me + away, count)}, device_id_type=MESH
            )
        pl.semaphore_wait(barrier, count - 1)

    @pl.when(step < batch)
    def _():
        held[...] = state_ref[0]

        @pl.loop(0, blocks, unroll=4)
        def _(index):
            at = pl.ds(pl.multiple_of(index * BLOCK, BLOCK), BLOCK)
            wide_fout = spread(fout_ref[0, at, :], expand_ref[...])
            em = em_ref[0, pl.ds(pl.multiple_of(index * 8, 8), 8), :]
            wide_em = spread(em, expand_ref[...])[0:1, :]
            b_rows = bc_ref[0, at, :STATE]
            c_rows = bc_ref[0, at, STATE:]
            scores = lax.dot_general(
                c_rows, b_rows, (((1,), (1,)), ((), ())), preferred_element_type=F32
            )
            mixing = jnp.where(rows >= cols, scores, 0.0).astype(BF16)
            left = jnp.concatenate([c_rows, mixing], axis=1)
            total = jnp.zeros((BLOCK, 128), F32)
            for start in range(0, width, tile):
                cut = slice(start, start + tile)
                scaled = scaled_ref[0, at, cut]
                e = wide_em[:, cut]
                entering = e * held[:, cut]
                right[:STATE, cut] = entering.astype(BF16)
                right[STATE:, cut] = scaled
                y = jnp.dot(left, right[:, cut], preferred_element_type=F32)
                added = lax.dot_general(
                    b_rows, scaled, (((0,), (0,)), ((), ())), preferred_element_type=F32
                )
                held[:, cut] = e * (entering + added)
                gated = y * wide_fout[:, cut] * silu(gate_ref[0, at, cut].astype(F32))
                gated_all[step, at, cut] = gated
                squared = gated * gated
                for piece in range(0, tile, 128):
                    total = total + squared[:, piece : piece + 128]
            column = jnp.sum(total, axis=1, keepdims=True)
            sums[...] += jnp.where(lane == step * blocks + index, column, 0.0)

    @pl.when(step == batch - 1)
    def _():
        for send in sends():
            send.start()

    @pl.when(step == batch)
    def _():
        for send in sends():
            send.wait()

    @pl.when(step >= batch)
    def _():
        whole_sq = sums[...]
        for away in range(1, count):
            whole_sq = whole_sq + others[away - 1]
        scale = lax.rsqrt(whole_sq / DI + epsilon)

        @pl.loop(0, blocks, unroll=4)
        def _(index):
            at = pl.ds(pl.multiple_of(index * BLOCK, BLOCK), BLOCK)
            here = (step - batch) * blocks + index
            column = jnp.sum(jnp.where(lane == here, scale, 0.0), axis=1, keepdims=True)
            for start in range(0, width, tile):
                cut = slice(start, start + tile)
                out_ref[0, at, cut] = (
                    gated_all[step - batch, at, cut] * column * gain_ref[:, cut]
                ).astype(BF16)


def one_batch(shape):
    return pl.BlockSpec((1,) + tuple(shape[1:]), lambda b: (b,) + (0,) * (len(shape) - 1))


def whole(shape):
    return pl.BlockSpec(tuple(shape), lambda b: (0,) * len(shape))


def per_device(
    hidden_in, gate_proj, value_proj, bc_proj, step_proj,
    value_conv, bc_conv, step_bias, log_rate, norm_gain,
):
    batch, length, model_width = hidden_in.shape
    heads = step_proj.shape[1]
    width = value_proj.shape[1]
    narrow = bc_proj.shape[1]
    blocks = length // BLOCK
    tp = lax.axis_size("tp")
    tile = tile_of(width)
    flat = hidden_in.reshape(-1, model_width)
    halo_in = shifted(hidden_in[:, length - PAD :, :], "seq", 1)

    small = jnp.concatenate([bc_proj, step_proj], axis=1)
    small_pre = jnp.dot(flat, small, preferred_element_type=F32)
    step_pre = small_pre[:, narrow:].reshape(batch, length, heads)
    bc_part = small_pre[:, :narrow].astype(BF16).reshape(batch, length, narrow)
    bc_halo = jnp.dot(
        halo_in.reshape(-1, model_width), bc_proj, preferred_element_type=F32
    ).astype(BF16).reshape(batch, PAD, narrow)
    bc_part = jnp.concatenate([bc_halo, bc_part], axis=1).reshape(-1, narrow)
    hbm = pl.BlockSpec(memory_space=pl.ANY)
    padded = PAD + length
    value_pre, bc_pre = pl.pallas_call(
        value_kernel,
        grid=(width // tile,),
        out_shape=(
            jax.ShapeDtypeStruct((batch, padded, width), BF16),
            jax.ShapeDtypeStruct((batch * padded, narrow * tp), BF16),
        ),
        in_specs=[hbm, hbm, hbm, pl.BlockSpec((model_width, tile), lambda j: (0, j))],
        out_specs=[
            pl.BlockSpec((batch, padded, tile), lambda j: (0, 0, j)),
            pl.BlockSpec((batch * padded, narrow * tp), lambda j: (0, 0)),
        ],
        scratch_shapes=[
            pltpu.VMEM((batch, padded, model_width), BF16),
            pltpu.VMEM((tp, batch * padded, narrow), BF16),
            pltpu.SemaphoreType.DMA((2 * batch + 1,)),
            pltpu.SemaphoreType.DMA((tp - 1,)),
            pltpu.SemaphoreType.DMA((tp - 1,)),
        ],
        compiler_params=pltpu.CompilerParams(
            vmem_limit_bytes=24 << 20, collective_id=0, has_side_effects=True
        ),
        name="value",
    )(hidden_in, halo_in, bc_part, value_proj)
    bc_pre = bc_pre.reshape(batch, padded, narrow * tp)

    lanes = lax.broadcasted_iota(jnp.int32, (2 * heads, width), 1) // HEAD_DIM
    owner = lax.broadcasted_iota(jnp.int32, (2 * heads, width), 0) % heads
    expand = (lanes == owner).astype(BF16)
    bias = step_bias.reshape(1, heads)
    rate = log_rate.reshape(1, heads)

    ins = (value_pre, bc_pre, step_pre)
    fixed = (value_conv, bc_conv, bias, rate, expand)
    outs = (
        jax.ShapeDtypeStruct((batch, length, width), BF16),
        jax.ShapeDtypeStruct((batch, length, 2 * STATE), BF16),
        jax.ShapeDtypeStruct((batch, length, heads), F32),
        jax.ShapeDtypeStruct((batch, blocks * 8, heads), F32),
        jax.ShapeDtypeStruct((batch, STATE, width), BF16),
        jax.ShapeDtypeStruct((batch, 8, width), F32),
    )
    scaled, bc, fout, em, local_state, decay = pl.pallas_call(
        state_kernel,
        grid=(batch,),
        out_shape=outs,
        in_specs=[one_batch(a.shape) for a in ins] + [whole(a.shape) for a in fixed],
        out_specs=[one_batch(a.shape) for a in outs],
        scratch_shapes=[
            pltpu.VMEM((BLOCK + PAD, width), F32),
            pltpu.VMEM((BLOCK + PAD, 2 * STATE), F32),
            pltpu.VMEM((8, heads), F32),
            pltpu.VMEM((STATE, width), F32),
        ],
        compiler_params=pltpu.CompilerParams(vmem_limit_bytes=24 << 20),
        cost_estimate=pl.CostEstimate(
            flops=1 << 30, bytes_accessed=8 << 20, transcendentals=1 << 21
        ),
        name="state",
    )(*ins, *fixed)

    span = jnp.concatenate([decay[:, 0, :], decay[: 8 - batch, 1, :]], axis=0)
    span = jnp.pad(span, ((0, 8 - span.shape[0]), (0, 0)))
    chips = lax.axis_size("seq") // 2
    rounds = max(1, (chips - 1).bit_length())
    half = STATE // 2
    moves = 3 + 2 * rounds
    once = pl.Buffered(1)
    gate_pre, before = pl.pallas_call(
        gate_kernel,
        grid=(width // tile,),
        out_shape=(
            jax.ShapeDtypeStruct((batch * length, width), BF16),
            jax.ShapeDtypeStruct((batch, STATE, width), F32),
        ),
        in_specs=[
            pl.BlockSpec(flat.shape, lambda j: (0, 0), pipeline_mode=once),
            pl.BlockSpec((model_width, tile), lambda j: (0, j)),
            pl.BlockSpec(local_state.shape, lambda j: (0, 0, 0), pipeline_mode=once),
            pl.BlockSpec(span.shape, lambda j: (0, 0), pipeline_mode=once),
        ],
        out_specs=[
            pl.BlockSpec((batch * length, tile), lambda j: (0, j)),
            pl.BlockSpec((batch, STATE, width), lambda j: (0, 0, 0)),
        ],
        scratch_shapes=[
            pltpu.VMEM((batch, STATE, width), BF16),
            pltpu.VMEM((8, width), F32),
            pltpu.VMEM((rounds, batch, half, width), BF16),
            pltpu.VMEM((rounds, 8, width), F32),
            pltpu.VMEM((rounds, batch, half, width), BF16),
            pltpu.VMEM((rounds, 8, width), F32),
            pltpu.VMEM((batch, STATE, width), BF16),
            pltpu.VMEM((batch, half, width), BF16),
            pltpu.VMEM((8, width), F32),
            pltpu.SemaphoreType.DMA((moves,)),
            pltpu.SemaphoreType.DMA((moves,)),
        ],
        compiler_params=pltpu.CompilerParams(
            vmem_limit_bytes=26 << 20, collective_id=1, has_side_effects=True
        ),
        name="gate",
    )(flat, gate_proj, local_state, span)
    gate_pre = gate_pre.reshape(batch, length, width)

    ins = (scaled, bc, fout, em, before, gate_pre)

    def clamped(shape):
        return pl.BlockSpec(
            (1,) + tuple(shape[1:]), lambda s: (jnp.minimum(s, batch - 1), 0, 0)
        )

    gain = norm_gain.reshape(1, width)
    return pl.pallas_call(
        output_kernel,
        grid=(2 * batch,),
        out_shape=jax.ShapeDtypeStruct((batch, length, width), BF16),
        in_specs=[clamped(a.shape) for a in ins] + [whole(expand.shape), whole(gain.shape)],
        out_specs=pl.BlockSpec(
            (1, length, width), lambda s: (jnp.maximum(s - batch, 0), 0, 0)
        ),
        scratch_shapes=[
            pltpu.VMEM((STATE, width), F32),
            pltpu.VMEM((STATE + BLOCK, width), BF16),
            pltpu.VMEM((batch, length, width), F32),
            pltpu.VMEM((BLOCK, 128), F32),
            pltpu.VMEM((tp - 1, BLOCK, 128), F32),
            pltpu.SemaphoreType.DMA((tp - 1,)),
            pltpu.SemaphoreType.DMA((tp - 1,)),
        ],
        compiler_params=pltpu.CompilerParams(
            vmem_limit_bytes=30 << 20, collective_id=2, has_side_effects=True
        ),
        name="outputs",
    )(*ins, expand, gain)


def solution(mesh):
    return jax.shard_map(
        per_device,
        mesh=mesh,
        in_specs=(
            P(None, "seq", None),
            P(None, "tp"),
            P(None, "tp"),
            P(None, "tp"),
            P(None, "tp"),
            P(None, "tp"),
            P(),
            P("tp"),
            P("tp"),
            P("tp"),
        ),
        out_specs=P(None, "seq", "tp"),
        check_vma=False,
    )
```

profile of v0, /device:TPU:24, one launch (start us, length us, event | category | flops | bytes accessed | tf_op | source)
XLA Modules:
  0.0 136.2 jit_solution(7050065458380306178)
XLA Ops:
  0.0 0.0 copy-start.8
  0.0 0.9 slice.16
  0.9 1.9 %collective-permute-start = (bf16[2,16,2560]{2,1,0:T(8,128)(2,1)S(1)}, bf16[2,16,2560]{2,1,0:T(8,128)(2,1)S(1)}, u32[]{:S(2)}, u32[]{:S(2)}) collective-permute-start(bf16[2,16,2560]{2,1,0:T(8,128)(2,1)S(1)} %slice.16), channel_id=1, source_target_pairs={{0,8},{8,16},{16,24},{24,32},{32,40},{40,48},{48,56},{56,64},{64,7... | collective-permute-start | bytes 491528 | tf_op jit(solution)/shard_map/ppermute | solution.py:25
  2.9 0.0 copy-start.7
  2.9 4.3 %convolution_bitcast_fusion = f32[1024,42]{0,1:T(8,128)S(1)} fusion(bf16[1024,2560]{1,0:T(8,128)(2,1)} %bitcast.19, bf16[2560,10]{0,1:T(8,128)(2,1)} %param.14, bf16[2560,32]{0,1:T(8,128)(2,1)} %param.13), kind=kOutput, calls=%fused_computation | convolution fusion | flops 220631040 | bytes 5629952 | tf_op jit(solution)/shard_map/dot_general | solution.py:409
  7.2 0.0 slice-start
  7.3 0.0 copy-done.8
  7.3 0.2 copy.25
  7.5 0.2 copy.22
  7.7 0.1 fusion.3.expand_ref
  7.8 1.9 %collective-permute-done.halo_ref = bf16[2,16,2560]{2,1,0:T(8,128)(2,1)S(1)} collective-permute-done((bf16[2,16,2560]{2,1,0:T(8,128)(2,1)S(1)}, bf16[2,16,2560]{2,1,0:T(8,128)(2,1)S(1)}, u32[]{:S(2)}, u32[]{:S(2)}) %collective-permute-start) | collective-permute-done | bytes 163872 | tf_op jit(solution)/shard_map/ppermute | solution.py:25
  9.7 0.0 copy-done.7
  9.7 0.2 convolution_convert_fusion
  9.9 0.1 pad_maximum_fusion
  9.9 0.0 copy-start
  10.0 2.5 %copy-done = bf16[2,512,2560]{2,1,0:T(8,128)(2,1)S(1)} copy-done((bf16[2,512,2560]{2,1,0:T(8,128)(2,1)S(1)}, bf16[2,512,2560]{2,1,0:T(8,128)(2,1)}, u32[]{:S(2)}) %copy-start) | copy-done | bytes 5242904
  12.4 0.0 copy-start.1
  12.4 1.9 %copy-done.1 = bf16[2560,640]{1,0:T(8,128)(2,1)S(1)} copy-done((bf16[2560,640]{1,0:T(8,128)(2,1)S(1)}, bf16[2560,640]{1,0:T(8,128)(2,1)}, u32[]{:S(2)}) %copy-start.1) | copy-done | bytes 3276824
  14.4 0.0 copy-start.3
  14.4 0.0 copy-start.4
  14.4 0.0 copy-start.5
  14.4 0.0 copy-start.6
  14.4 0.0 slice-start.1
  14.4 57.4 %value.1 = (bf16[2,528,640]{2,1,0:T(8,128)(2,1)S(1)}, bf16[1056,256]{1,0:T(8,128)(2,1)S(1)}) custom-call(bf16[2,512,2560]{2,1,0:T(8,128)(2,1)S(1)} %copy-done, bf16[2,16,2560]{2,1,0:T(8,128)(2,1)S(1)} %collective-permute-done.halo_ref, bf16[1056,32]{1,0:T(8,128)(2,1)S(1)} %bitcast.24, bf16[2560,640]{1,0:T(8,128)(2,1)S(1)} %copy-done.1), custom_call_target="tpu_custom_call" | custom-call | tf_op jit(solution)/shard_map/value/pallas_call | solution.py:418
  71.8 0.0 copy-start.2
  71.8 0.0 copy-done.3
  71.8 0.0 copy-done.4
  71.8 0.0 copy-done.5
  71.8 0.0 copy-done.6
  71.8 10.4 %state.1 = (bf16[2,512,640]{2,1,0:T(8,128)(2,1)S(1)}, bf16[2,512,256]{2,1,0:T(8,128)(2,1)S(1)}, f32[2,512,10]{2,1,0:T(8,128)S(1)}, f32[2,64,10]{2,1,0:T(8,128)S(...) custom-call(bf16[2,528,640]{2,1,0:T(8,128)(2,1)S(1)} %get-tuple-element.15.pre_ref, ...), custom_call_target="tpu_custom_call" | custom-call | flops 1073741824 | bytes 8388608 | tf_op jit(solution)/shard_map/state/pallas_call | solution.py:460
  82.3 0.0 slice-done
  82.3 0.0 slice-done.1
  82.3 0.0 copy-done.2
  82.3 33.4 %gate.1 = (bf16[1024,640]{1,0:T(8,128)(2,1)S(1)}, f32[2,128,640]{2,1,0:T(8,128)S(1)}) custom-call(bf16[1024,2560]{1,0:T(8,128)(2,1)S(1)} %bitcast.22, bf16[2560,640]{1,0:T(8,128)(2,1)S(1)} %copy-done.2, bf16[2,128,640]{2,1,0:T(8,128)(2,1)S(1)} %get-tuple-element.21.local_ref, f32[8,640]{1,0:T(8,128)S(1)} %select_maximum_fusion.span_ref), custom_call_target="tpu_custom_call" | custom-call | tf_op jit(solution)/shard_map/gate/pallas_call | solution.py:486
  115.8 19.3 %outputs.1 = bf16[2,512,640]{2,1,0:T(8,128)(2,1)S(1)} custom-call(bf16[2,512,640]{2,1,0:T(8,128)(2,1)S(1)} %get-tuple-element.17.scaled_ref, bf16[2,512,256]{2,1,0:T(8,128)(2,1)S(1)} %get-tuple-element.18.bc_ref, f32[2,512,10]{2,1,0:T(8,128)S(1)} %get-tuple-element.19.fout_ref, f32[2,64,10]{2,1,0:T(8,128)S(1)} %get-tuple-element.20.em_ref, ...), custom_call_target="tpu_custom_call" | custom-call | tf_op jit(solution)/shard_map/outputs/pallas_call | solution.py:531
  135.1 1.1 copy.27
  (11 shorter events, 0.1 us)
Async XLA Ops:
  0.0 7.3 %copy-start.8 = (f32[640]{0:T(1024)S(1)}, f32[640]{0:T(1024)}, u32[]{:S(2)}) copy-start(f32[640]{0:T(1024)} %param.19) | copy-start | bytes 7684
  0.9 8.7 %collective-permute-start = (bf16[2,16,2560]{2,1,0:T(8,128)(2,1)S(1)}, bf16[2,16,2560]{2,1,0:T(8,128)(2,1)S(1)}, u32[]{:S(2)}, u32[]{:S(2)}) collective-permute-start(bf16[2,16,2560]{2,1,0:T(8,128)(2,1)S(1)} %slice.16), channel_id=1, source_target_pairs={{0,8},{8,16},{16,24},{24,32},{32,40},{40,48},{48,56},{56,64},{64,7... | collective-permute-start | bytes 491528 | tf_op jit(solution)/shard_map/ppermute | solution.py:25
  2.9 6.8 %copy-start.7 = (bf16[2560,32]{0,1:T(8,128)(2,1)S(1)}, bf16[2560,32]{0,1:T(8,128)(2,1)}, u32[]{:S(2)}) copy-start(bf16[2560,32]{0,1:T(8,128)(2,1)} %param.13) | copy-start | bytes 491524
  7.2 75.1 %slice-start = ((s8[5242880]{0:T(1024)(128)(4,1)}), s8[1048576]{0:T(1024)(128)(4,1)S(1)}, s32[]{:S(2)}) async-start(s8[5242880]{0:T(1024)(128)(4,1)} %bitcast.20), calls=%async_computation | async-start | bytes 2097152
  9.9 2.5 %copy-start = (bf16[2,512,2560]{2,1,0:T(8,128)(2,1)S(1)}, bf16[2,512,2560]{2,1,0:T(8,128)(2,1)}, u32[]{:S(2)}) copy-start(bf16[2,512,2560]{2,1,0:T(8,128)(2,1)} %hidden_ref.1) | copy-start | bytes 15728644
  12.4 1.9 %copy-start.1 = (bf16[2560,640]{1,0:T(8,128)(2,1)S(1)}, bf16[2560,640]{1,0:T(8,128)(2,1)}, u32[]{:S(2)}) copy-start(bf16[2560,640]{1,0:T(8,128)(2,1)} %weight_ref.2) | copy-start | bytes 9830404
  14.4 57.4 %copy-start.3 = (f32[4,640]{1,0:T(4,128)S(1)}, f32[4,640]{1,0:T(4,128)}, u32[]{:S(2)}) copy-start(f32[4,640]{1,0:T(4,128)} %kernel_ref.1) | copy-start | bytes 30724
  14.4 57.4 %copy-start.4 = (f32[4,256]{1,0:T(4,128)S(1)}, f32[4,256]{1,0:T(4,128)}, u32[]{:S(2)}) copy-start(f32[4,256]{1,0:T(4,128)} %bc_kernel_ref.1) | copy-start | bytes 12292
  14.4 57.4 %copy-start.5 = (f32[10]{0:T(128)S(1)}, f32[10]{0:T(128)}, u32[]{:S(2)}) copy-start(f32[10]{0:T(128)} %param.17) | copy-start | bytes 124
  14.4 57.5 %copy-start.6 = (f32[10]{0:T(128)S(1)}, f32[10]{0:T(128)}, u32[]{:S(2)}) copy-start(f32[10]{0:T(128)} %param.18) | copy-start | bytes 124
  14.4 67.9 %slice-start.1 = ((s8[5242880]{0:T(1024)(128)(4,1)}), s8[4194304]{0:T(1024)(128)(4,1)S(1)}, s32[]{:S(2)}) async-start(s8[5242880]{0:T(1024)(128)(4,1)} %bitcast.20), calls=%async_computation.1 | async-start | bytes 8388608
  71.8 10.5 %copy-start.2 = (bf16[2560,640]{1,0:T(8,128)(2,1)S(1)}, bf16[2560,640]{1,0:T(8,128)(2,1)}, u32[]{:S(2)}) copy-start(bf16[2560,640]{1,0:T(8,128)(2,1)} %weight_ref.3) | copy-start | bytes 9830404
where the time goes:
time: 136 us
  Pallas kernels  121 us (89%)
  local copies, waits for them, and re-layouts  6.9 us (5%)
  matrix products  4.45 us (3%)
  starting transfers between devices  1.92 us (1%)
  waiting for transfers between devices  1.89 us (1%)
    pallas_call x1, Pallas kernels, per_device(): pl.pallas_call(value_kernel, grid=(width // tile,), out_shape=(jax.ShapeD...  57.4 us
    pallas_call x1, Pallas kernels, per_device(): pl.pallas_call(gate_kernel, grid=(width // tile,), out_shape=(jax.ShapeDt...  33.4 us
    pallas_call x1, Pallas kernels, per_device(): pl.pallas_call(output_kernel, grid=(2 * batch,), out_shape=jax.ShapeDtype...  19.3 us
    pallas_call x1, Pallas kernels, per_device(): pl.pallas_call(state_kernel, grid=(batch,), out_shape=outs, in_specs=[one...  10.4 us
    unnamed x23, local copies, waits for them, and re-layouts  5.51 us
    dot_general x1, matrix products, per_device(): small_pre = jnp.dot(flat, small, preferred_element_type=F32)  4.28 us
  transfers between devices with their start and end apart: 1, of which 1 were waited for; matrix products, arithmetic and copies ran while one was open for 4% of the time, Pallas kernels for 0%

commit v1 on v0

v1 whole, which is shorter than its diff:
```python
import jax
import jax.numpy as jnp
from jax import lax
from jax.experimental import pallas as pl
from jax.experimental.pallas import tpu as pltpu
from jax.sharding import PartitionSpec as P

DI = 5120
HEAD_DIM = 64
STATE = 128
CONV = 4
BLOCK = 128
LANES = 128
PAD = 16
HALO = 8
TILE = 256
MESH = pl.DeviceIdType.MESH

epsilon = 1e-05
F32 = jnp.float32
BF16 = jnp.bfloat16


def silu(x):
    return x * (1.0 / (1.0 + jnp.exp(-x)))


def halves(x):
    high = x.astype(BF16)
    low = (x - high.astype(F32)).astype(BF16)
    return jnp.concatenate([high, low], axis=1)


def dot_nt(a, b):
    return lax.dot_general(a, b, (((1,), (1,)), ((), ())), preferred_element_type=F32)


def mixer_kernel(
    hidden_ref, value_ref, gate_ref, small_ref, conv_ref, bc_conv_ref,
    bias_ref, rate_ref, expand_ref,
    gated_ref, scale_ref,
    rows, weights, small_pre, bc_wide, fin, fout, ends, logs, pair_logs, chip_logs,
    all_logs, early, late, pre, gates, scaled, right, other,
    local, pair, sent, got, prefix, owned, owned_pair, entering, sums, others,
    load_sem, halo_sem, log_sem, log_send, log_recv, early_send, early_recv,
    late_send, late_recv, pair_sem, out_send, out_recv, back_send, back_recv,
    swap_sem, sum_send, sum_recv,
):
    batch, length, _ = hidden_ref.shape
    width = value_ref.shape[1]
    blocks = length // BLOCK
    total_blocks = batch * blocks
    narrow = early.shape[1]
    late_len = late.shape[2] // batch
    early_len = early.shape[2] // batch
    me = lax.axis_index("tp")
    ring = lax.axis_size("tp")
    place = lax.axis_index("seq")
    devices = lax.axis_size("seq")
    chips = devices // 2
    core = lax.rem(place, 2)
    chip = place // 2
    partner = place + 1 - 2 * core
    after = lax.rem(place + 1, devices)
    before = lax.rem(place + devices - 1, devices)
    half = STATE // 2
    mine = pl.ds(pl.multiple_of(core * half, half), half)

    def chip_at(away):
        return lax.rem(chip + away, chips)

    def tp_at(away):
        return lax.rem(me + away, ring)

    def remote(source, target, send, recv, **device):
        return pltpu.make_async_remote_copy(
            src_ref=source, dst_ref=target, send_sem=send, recv_sem=recv,
            device_id=device, device_id_type=MESH,
        )

    chunk = length // 2
    loads = []
    for b in range(batch):
        for part in range(2):
            loads.append(pltpu.make_async_copy(
                hidden_ref.at[b, pl.ds(part * chunk, chunk)],
                rows.at[b, pl.ds(PAD + part * chunk, chunk)], load_sem.at[2 * b + part],
            ))
    gate_load = pltpu.make_async_copy(
        gate_ref, weights.at[:, pl.ds(width, width)], load_sem.at[2 * batch]
    )
    value_load = pltpu.make_async_copy(
        value_ref, weights.at[:, pl.ds(0, width)], load_sem.at[2 * batch + 1]
    )
    for load in loads:
        load.start()
    gate_load.start()
    value_load.start()

    barrier = pltpu.get_barrier_semaphore()
    for device in (after, before, partner):
        pl.semaphore_signal(barrier, inc=1, device_id={"seq": device}, device_id_type=MESH)
    for away in range(1, ring):
        pl.semaphore_signal(
            barrier, inc=1, device_id={"tp": tp_at(away)}, device_id_type=MESH
        )
    for away in range(1, chips):
        pl.semaphore_signal(
            barrier, inc=1, device_id={"seq": 2 * chip_at(away) + core}, device_id_type=MESH
        )

    for b in range(batch):
        rows[b, 0:HALO, :] = jnp.zeros((HALO, rows.shape[2]), BF16)
        small_pre[b, 0:LANES, :] = jnp.zeros((LANES, LANES), F32)
    for b in range(batch):
        for part in range(2):
            loads[2 * b + part].wait()
            at = slice(part * chunk, (part + 1) * chunk)
            small_pre[b, LANES + at.start : LANES + at.stop, :] = dot_nt(
                rows[b, PAD + at.start : PAD + at.stop, :], small_ref[...]
            )
    pl.semaphore_wait(barrier, 3 + (ring - 1) + (chips - 1))

    halo = remote(
        rows.at[:, pl.ds(PAD + length - HALO, HALO)], rows.at[:, pl.ds(PAD - HALO, HALO)],
        halo_sem.at[0], halo_sem.at[1], seq=after,
    )
    halo.start()

    taps = bc_conv_ref[pl.ds(pl.multiple_of(me * narrow, narrow), narrow), :]

    def bc_conv(x):
        total = taps[:, CONV - 1 : CONV] * x
        for k in range(1, CONV):
            total = total + taps[:, CONV - 1 - k : CONV - k] * pltpu.roll(x, k, 1)
        return silu(total).astype(BF16)

    def transpose_bc(b, piece):
        at = slice(piece * LANES, (piece + 1) * LANES)
        flipped = jnp.transpose(small_pre[b, at, :])[0:narrow, :]
        bc_wide[b, :, at] = flipped.astype(BF16).astype(F32)

    for b in range(batch):
        for piece in range(1, 1 + length // LANES):
            transpose_bc(b, piece)
        done = bc_conv(bc_wide[b, :, LANES : LANES + length])
        early[me, :, b * early_len : (b + 1) * early_len] = done[:, late_len:]

    def ring_copies(slots, send, recv, clockwise, step):
        index = step if clockwise else ring // 2 + step
        source = tp_at(ring - step) if clockwise else tp_at(step)
        target = tp_at(1) if clockwise else tp_at(ring - 1)
        return remote(
            slots.at[source], slots.at[source], send.at[index], recv.at[index], tp=target
        )

    early_steps = (ring // 2, ring - 1 - ring // 2)
    late_steps = (ring - 1 - ring // 2, ring // 2)

    def ring_start(slots, send, recv, steps, step):
        for clockwise in (True, False):
            if step < steps[0 if clockwise else 1]:
                ring_copies(slots, send, recv, clockwise, step).start()

    def ring_next(slots, send, recv, steps, step):
        for clockwise in (True, False):
            if step < steps[0 if clockwise else 1]:
                ring_copies(slots, send, recv, clockwise, step).wait_recv()
        ring_start(slots, send, recv, steps, step + 1)

    def ring_finish(slots, send, recv, steps):
        for clockwise in (True, False):
            for step in range(steps[0 if clockwise else 1]):
                ring_copies(slots, send, recv, clockwise, step).wait_send()

    early_ring = (early, early_send, early_recv, early_steps)
    late_ring = (late, late_send, late_recv, late_steps)
    ring_start(*early_ring, 0)

    row = lax.broadcasted_iota(jnp.int32, (BLOCK, BLOCK), 0)
    col = lax.broadcasted_iota(jnp.int32, (BLOCK, BLOCK), 1)
    triangle = jnp.where(row >= col, 1.0, 0.0).astype(F32)
    ms, mos, totals = [], [], []
    for b in range(batch):
        offset = jnp.zeros((1, LANES), F32)
        for k in range(blocks):
            step_pre = small_pre[b, LANES + k * BLOCK : LANES + (k + 1) * BLOCK, :] + bias_ref[...]
            steps = jnp.maximum(step_pre, 0.0) + jnp.log1p(jnp.exp(-jnp.abs(step_pre)))
            cumulative = jnp.dot(
                triangle, -steps * rate_ref[...],
                precision=lax.Precision.HIGHEST, preferred_element_type=F32,
            )
            last = cumulative[BLOCK - 1 : BLOCK, :]
            mid = 0.5 * last
            fin[b * blocks + k] = halves(jnp.exp(mid - cumulative) * steps)
            fout[b * blocks + k] = halves(jnp.exp(cumulative - mid))
            ms.append(mid)
            mos.append(mid + offset)
            offset = offset + last
        totals.append(offset)
    table = jnp.exp(jnp.concatenate(ms + mos, axis=0))
    ends[...] = jnp.dot(halves(table), expand_ref[...], preferred_element_type=F32)
    logs[...] = jnp.concatenate(totals + [jnp.zeros((8 - batch, LANES), F32)], axis=0)
    pair_log = remote(logs, pair_logs, log_sem.at[0], log_sem.at[1], seq=partner)
    pair_log.start()

    def log_copies(away):
        return remote(
            chip_logs, all_logs.at[chip], log_send.at[away - 1], log_recv.at[away - 1],
            seq=2 * chip_at(away) + core,
        )

    def gate_part(b, product):
        return silu(product.astype(BF16).astype(F32))

    def tile_of(index):
        cut = slice(index * TILE, (index + 1) * TILE)

        @pl.loop(0, batch)
        def _(b):
            if cut.start >= width:
                product = jnp.dot(
                    rows[b, PAD : PAD + length, :], weights[:, cut], preferred_element_type=F32
                )
                gates[b, :, cut.start - width : cut.stop - width] = gate_part(b, product)
            else:
                product = jnp.dot(rows[b], weights[:, cut], preferred_element_type=F32)
                inner = min(TILE, width - cut.start)
                pre[b, :, cut.start : cut.start + inner] = (
                    product[:, :inner].astype(BF16).astype(F32)
                )
                if inner < TILE:
                    gates[b, :, 0 : TILE - inner] = gate_part(b, product[PAD:, inner:])

    tiles = 2 * width // TILE
    value_tiles = -(-width // TILE)
    gate_load.wait()
    tile_of(tiles - 1)

    halo.wait()

    @pl.when(place == 0)
    def _():
        for b in range(batch):
            rows[b, 0:PAD, :] = jnp.zeros((PAD, rows.shape[2]), BF16)

    for b in range(batch):
        small_pre[b, LANES - PAD : LANES, :] = dot_nt(rows[b, 0:PAD, :], small_ref[...])
        transpose_bc(b, 0)
        done = bc_conv(bc_wide[b, :, 0 : LANES + late_len])
        late[me, :, b * late_len : (b + 1) * late_len] = done[:, LANES:]
    ring_start(*late_ring, 0)
    pair_log.wait()
    chip_logs[...] = logs[...] + pair_logs[...]
    all_logs[chip] = logs[...] + pair_logs[...]
    for away in range(1, chips):
        log_copies(away).start()

    for index in range(value_tiles, tiles - 1):
        tile_of(index)
    ring_next(*early_ring, 0)
    value_load.wait()
    tile_of(0)
    ring_next(*late_ring, 0)
    tile_of(1)
    ring_next(*early_ring, 1)
    ring_next(*late_ring, 1)
    for index in range(2, value_tiles):
        tile_of(index)
    ring_next(*early_ring, 2)
    ring_next(*late_ring, 2)

    for b in range(batch):
        for k in range(blocks):
            base = PAD + k * BLOCK - CONV + 1
            wide = jnp.dot(fin[b * blocks + k], expand_ref[...], preferred_element_type=F32)
            for start in range(0, width, LANES):
                cut = slice(start, start + LANES)
                x = conv_ref[0:1, cut] * pre[b, base : base + BLOCK, cut]
                for tap in range(1, CONV):
                    x = x + conv_ref[tap : tap + 1, cut] * pre[
                        b, base + tap : base + tap + BLOCK, cut
                    ]
                right[b * blocks + k, STATE:, cut] = (silu(x) * wide[:, cut]).astype(BF16)

    ring_next(*early_ring, 3)
    ring_next(*late_ring, 3)

    def bc_block(b, k, first):
        at = k * BLOCK
        if at < late_len:
            part = late[first : first + ring // 2, :, b * late_len + at : b * late_len + at + BLOCK]
        else:
            at += b * early_len - late_len
            part = early[first : first + ring // 2, :, at : at + BLOCK]
        return part.reshape(STATE, BLOCK)

    for b in range(batch):
        held = jnp.zeros((STATE, width), F32)
        for k in range(blocks):
            g = b * blocks + k
            e = ends[g : g + 1, :]
            ahead = e * held
            right[g, :STATE, :] = ahead.astype(BF16)
            added = jnp.dot(
                bc_block(b, k, 0), right[g, STATE:, :], preferred_element_type=F32
            )
            held = e * (ahead + added)
        local[b] = held.astype(BF16)

    pair_copy = remote(local, pair, pair_sem.at[0], pair_sem.at[1], seq=partner)
    pair_copy.start()
    for away in range(1, chips):
        log_copies(away).wait()
    own_end = jnp.exp(logs[...])
    pair_end = jnp.exp(pair_logs[...])
    wide_ends = jnp.dot(
        halves(jnp.concatenate([own_end, pair_end], axis=0)), expand_ref[...],
        preferred_element_type=F32,
    )
    low = chip < chips // batch
    spans = jnp.concatenate(
        [jnp.where(low, all_logs[i, 0:1, :], all_logs[i, 1:2, :]) for i in range(chips)], axis=0
    )
    spans = jnp.dot(halves(jnp.exp(spans)), expand_ref[...], preferred_element_type=F32)

    def out_copies(away):
        peer = chip_at(away)
        return remote(
            sent.at[peer], got.at[chip], out_send.at[away - 1], out_recv.at[away - 1],
            seq=2 * peer + core,
        )

    def back_copies(away):
        peer = chip_at(away)
        return remote(
            prefix.at[peer], owned.at[chip], back_send.at[away - 1], back_recv.at[away - 1],
            seq=2 * peer + core,
        )

    pair_copy.wait()
    groups = chips // batch
    for b in range(batch):
        own = local[b, mine, :].astype(F32)
        theirs = pair[b, mine, :].astype(F32)
        first = jnp.where(core == 0, own, theirs)
        second = jnp.where(core == 0, theirs, own)
        later = jnp.where(core == 0, wide_ends[8 + b : 9 + b, :], wide_ends[b : b + 1, :])
        both = (later * first + second).reshape(groups, half // groups, width)
        sent[b * groups : (b + 1) * groups] = both.astype(BF16)
    got[chip] = sent[chip]
    for away in range(1, chips):
        out_copies(away).start()

    def left_of(b, k):
        b_flat = bc_block(b, k, 0)
        c_rows = jnp.transpose(bc_block(b, k, ring // 2).astype(F32)).astype(BF16)
        return b_flat, c_rows

    for b in range(batch):
        for k in range(blocks):
            g = b * blocks + k
            at = slice(k * BLOCK, (k + 1) * BLOCK)
            b_flat, c_rows = left_of(b, k)
            scores = jnp.dot(c_rows, b_flat, preferred_element_type=F32)
            mixing = jnp.where(row >= col, scores, 0.0).astype(BF16)
            left = jnp.concatenate([c_rows, mixing], axis=1)
            scaled[g] = c_rows
            wide = jnp.dot(fout[g], expand_ref[...], preferred_element_type=F32)
            y = jnp.dot(left, right[g], preferred_element_type=F32)
            weighted = wide * gates[b, at, :]
            gated_ref[b, at, :] = y * weighted
            other[b, at, :] = weighted * ends[total_blocks + g : total_blocks + g + 1, :]

    for away in range(1, chips):
        out_copies(away).wait()
    running = jnp.zeros((half // groups, width), F32)
    for i in range(chips):
        prefix[i] = running.astype(BF16)
        if i + 1 < chips:
            running = spans[i : i + 1, :] * running + got[i].astype(F32)
    owned[chip] = prefix[chip]
    for away in range(1, chips):
        back_copies(away).start()
    ring_finish(*early_ring)
    ring_finish(*late_ring)
    for away in range(1, chips):
        back_copies(away).wait()
    swap = remote(owned, owned_pair, swap_sem.at[0], swap_sem.at[1], seq=partner)
    swap.start()
    swap.wait()

    for b in range(batch):
        at = slice(b * groups, (b + 1) * groups)
        own = owned[at].astype(F32).reshape(half, width)
        theirs = owned_pair[at].astype(F32).reshape(half, width)
        span = wide_ends[8 + b : 9 + b, :]
        for c in range(2):
            cut = slice(c * half, (c + 1) * half)
            full = jnp.where(core == c, own, theirs)
            moved = span * full + pair[b, cut, :].astype(F32)
            entering[b, cut, :] = jnp.where(core == 0, full, moved).astype(BF16)

    for b in range(batch):
        for k in range(blocks):
            g = b * blocks + k
            at = slice(k * BLOCK, (k + 1) * BLOCK)
            extra = jnp.dot(scaled[g], entering[b], preferred_element_type=F32)
            total = jnp.zeros((BLOCK, LANES), F32)
            for start in range(0, width, LANES):
                cut = slice(start, start + LANES)
                gated = gated_ref[b, at, cut] + other[b, at, cut] * extra[:, cut]
                gated_ref[b, at, cut] = gated
                total = total + gated * gated
            sums[g : g + 1, :] = jnp.sum(jnp.transpose(total), axis=0, keepdims=True)

    def sum_copies(away):
        return remote(
            sums, others.at[away - 1], sum_send.at[away - 1], sum_recv.at[away - 1],
            tp=tp_at(away),
        )

    for away in range(1, ring):
        sum_copies(away).start()
    for away in range(1, ring):
        sum_copies(away).wait()
    whole_sq = sums[...]
    for away in range(1, ring):
        whole_sq = whole_sq + others[away - 1]
    scale_ref[...] = lax.rsqrt(whole_sq / DI + epsilon)


def norm_kernel(gated_ref, scale_ref, gain_ref, out_ref):
    width = gated_ref.shape[2]
    step = pl.program_id(0)
    count = gated_ref.shape[1] // BLOCK
    for k in range(count):
        at = slice(k * BLOCK, (k + 1) * BLOCK)
        line = scale_ref[pl.ds(step * count + k, 1), :]
        column = jnp.transpose(jnp.broadcast_to(line, (BLOCK, LANES)))
        for start in range(0, width, LANES):
            cut = slice(start, start + LANES)
            out_ref[0, at, cut] = (
                gated_ref[0, at, cut] * column * gain_ref[:, cut]
            ).astype(BF16)


def per_device(
    hidden_in, gate_proj, value_proj, bc_proj, step_proj,
    value_conv, bc_conv, step_bias, log_rate, norm_gain,
):
    batch, length, model_width = hidden_in.shape
    heads = step_proj.shape[1]
    width = value_proj.shape[1]
    narrow = bc_proj.shape[1]
    blocks = length // BLOCK
    tp = lax.axis_size("tp")
    chips = lax.axis_size("seq") // 2
    total_blocks = batch * blocks
    half = STATE // 2
    groups = chips // batch
    late_len = BLOCK
    early_len = length - late_len

    tail = LANES - narrow - heads
    small = jnp.concatenate(
        [bc_proj.T, step_proj.T, jnp.zeros((tail, model_width), BF16)], axis=0
    )
    bias = jnp.pad(step_bias, (narrow, tail)).reshape(1, LANES)
    rate = jnp.pad(jnp.exp(log_rate), (narrow, tail)).reshape(1, LANES)
    lanes = lax.broadcasted_iota(jnp.int32, (2 * LANES, width), 1) // HEAD_DIM
    owner = lax.broadcasted_iota(jnp.int32, (2 * LANES, width), 0) % LANES - narrow
    expand = (lanes == owner).astype(BF16)

    hbm = pl.BlockSpec(memory_space=pltpu.HBM)
    vmem = pl.BlockSpec(memory_space=pltpu.VMEM)
    dma = pltpu.SemaphoreType.DMA
    gated, scale = pl.pallas_call(
        mixer_kernel,
        out_shape=(
            jax.ShapeDtypeStruct((batch, length, width), F32),
            jax.ShapeDtypeStruct((total_blocks, LANES), F32),
        ),
        in_specs=[hbm] * 3 + [vmem] * 6,
        out_specs=[vmem, vmem],
        scratch_shapes=[
            pltpu.VMEM((batch, PAD + length, model_width), BF16),
            pltpu.VMEM((model_width, 2 * width), BF16),
            pltpu.VMEM((batch, LANES + length, LANES), F32),
            pltpu.VMEM((batch, narrow, LANES + length), F32),
            pltpu.VMEM((total_blocks, BLOCK, 2 * LANES), BF16),
            pltpu.VMEM((total_blocks, BLOCK, 2 * LANES), BF16),
            pltpu.VMEM((2 * total_blocks, width), F32),
            pltpu.VMEM((8, LANES), F32),
            pltpu.VMEM((8, LANES), F32),
            pltpu.VMEM((8, LANES), F32),
            pltpu.VMEM((chips, 8, LANES), F32),
            pltpu.VMEM((tp, narrow, batch * early_len), BF16),
            pltpu.VMEM((tp, narrow, batch * late_len), BF16),
            pltpu.VMEM((batch, PAD + length, width), F32),
            pltpu.VMEM((batch, length, width), F32),
            pltpu.VMEM((total_blocks, BLOCK, STATE), BF16),
            pltpu.VMEM((total_blocks, STATE + BLOCK, width), BF16),
            pltpu.VMEM((batch, length, width), F32),
            pltpu.VMEM((batch, STATE, width), BF16),
            pltpu.VMEM((batch, STATE, width), BF16),
            pltpu.VMEM((chips, half // groups, width), BF16),
            pltpu.VMEM((chips, half // groups, width), BF16),
            pltpu.VMEM((chips, half // groups, width), BF16),
            pltpu.VMEM((chips, half // groups, width), BF16),
            pltpu.VMEM((chips, half // groups, width), BF16),
            pltpu.VMEM((batch, STATE, width), BF16),
            pltpu.VMEM((total_blocks, LANES), F32),
            pltpu.VMEM((tp - 1, total_blocks, LANES), F32),
            dma((2 * batch + 2,)),
            dma((2,)),
            dma((2,)),
            dma((chips - 1,)),
            dma((chips - 1,)),
            dma((tp,)),
            dma((tp,)),
            dma((tp,)),
            dma((tp,)),
            dma((2,)),
            dma((chips - 1,)),
            dma((chips - 1,)),
            dma((chips - 1,)),
            dma((chips - 1,)),
            dma((2,)),
            dma((tp - 1,)),
            dma((tp - 1,)),
        ],
        compiler_params=pltpu.CompilerParams(
            vmem_limit_bytes=48 << 20, collective_id=0, has_side_effects=True
        ),
        name="mixer",
    )(
        hidden_in, value_proj, gate_proj, small, value_conv, bc_conv.T, bias, rate, expand,
    )

    part = 2 * BLOCK
    steps = length // part
    return pl.pallas_call(
        norm_kernel,
        grid=(batch * steps,),
        out_shape=jax.ShapeDtypeStruct((batch, length, width), BF16),
        in_specs=[
            pl.BlockSpec((1, part, width), lambda s: (s // steps, s % steps, 0)),
            pl.BlockSpec((total_blocks, LANES), lambda s: (0, 0)),
            pl.BlockSpec((1, width), lambda s: (0, 0)),
        ],
        out_specs=pl.BlockSpec((1, part, width), lambda s: (s // steps, s % steps, 0)),
        compiler_params=pltpu.CompilerParams(vmem_limit_bytes=12 << 20),
        name="norm",
    )(gated, scale, norm_gain.reshape(1, width))


def solution(mesh):
    return jax.shard_map(
        per_device,
        mesh=mesh,
        in_specs=(
            P(None, "seq", None),
            P(None, "tp"),
            P(None, "tp"),
            P(None, "tp"),
            P(None, "tp"),
            P(None, "tp"),
            P(),
            P("tp"),
            P("tp"),
            P("tp"),
        ),
        out_specs=P(None, "seq", "tp"),
        check_vma=False,
    )
```

time: 136 us -> 57.7 us (0.42)
  the two profiles are of different devices: /device:TPU:24 before, /device:TPU:1 now
where the time goes in v1:
time: 57.7 us; the launch traced here: 57.5 us
  Pallas kernels  53.1 us (92%)
  local copies, waits for them, and re-layouts  2.99 us (5%)
  other arithmetic  1.28 us (2%)
    pallas_call x1, Pallas kernels, per_device(): pl.pallas_call(mixer_kernel, out_shape=(jax.ShapeDtypeStruct((batch, leng...  51.2 us
    pallas_call x1, Pallas kernels, per_device(): pl.pallas_call(norm_kernel, grid=(batch * steps,), out_shape=jax.ShapeDty...  1.94 us

profile of v1, /device:TPU:1, one launch (start us, length us, event | category | flops | bytes accessed | tf_op | source)
XLA Modules:
  0.0 57.5 jit_solution(17538002530448491802)
XLA Ops:
  0.0 0.0 copy-start
  0.0 0.7 %exp.3 = f32[10]{0:T(128)S(1)} exponential(f32[10]{0:T(128)} %param.18) | non-fusion elementwise | bytes 80 | tf_op jit(solution)/shard_map/exp | solution.py:470
  0.7 0.1 pad.11.clone
  0.8 0.7 %pad_bitcast_fusion = (f32[1,128]{1,0:T(1,128)S(1)}, f32[1,128]{1,0:T(1,128)S(1)}) fusion(f32[10]{0:T(128)S(1)} %exp.3, f32[10]{0:T(128)} %param.17), kind=kLoop, calls=%fused_computation.13 | loop fusion | bytes 1104 | tf_op jit(solution)/shard_map/reshape | solution.py:470
  1.5 0.7 %reshape.11.gain_ref = f32[1,640]{1,0:T(1,128)S(1)} reshape(f32[640]{0:T(1024)} %param.19) | data formatting | bytes 5120 | tf_op jit(solution)/shard_map/reshape | solution.py:555
  2.2 0.8 %copy.11 = f32[4,256]{0,1:T(8,128)S(1)} copy(f32[4,256]{1,0:T(4,128)} %param.16) | data formatting | bytes 8192 | tf_op args[6]
  3.0 0.2 fusion.expand_ref
  3.2 1.1 %maximum_maximum_fusion.small_ref = bf16[128,2560]{1,0:T(8,128)(2,1)S(1)} fusion(bf16[10,2560]{1,0:T(8,128)(2,1)} %bitcast.9, bf16[32,2560]{1,0:T(8,128)(2,1)} %bitcast.8, bf16[128]{0:T(256)(128)(2,1)S(1)} %pad.11.clone), kind=kLoop, calls=%fused_computation | loop fusion | flops 1966080 | bytes 870656 | tf_op jit(solution)/shard_map/concatenate | solution.py:466
  4.3 0.0 copy-done
  4.3 51.2 %mixer.1 = (f32[2,512,640]{2,1,0:T(8,128)S(1)}, f32[8,128]{1,0:T(8,128)S(1)}) custom-call(bf16[2,512,2560]{2,1,0:T(8,128)(2,1)} %hidden_ref.1, bf16[2560,640]{1,0:T(8,128)(2,1)} %value_ref.1, bf16[2560,640]{1,0:T(8,128)(2,1)} %gate_ref.1, bf16[128,2560]{1,0:T(8,128)(2,1)S(1)} %maximum_maximum_fusion.small_ref, f32[4,640]{1,0:T(4,128)S(1)} %copy-done, ...), custom_call_target="tpu_custom_call" | custom-call | tf_op jit(solution)/shard_map/mixer/pallas_call | solution.py:478
  55.5 1.9 %norm.1 = bf16[2,512,640]{2,1,0:T(8,128)(2,1)} custom-call(f32[2,512,640]{2,1,0:T(8,128)S(1)} %get-tuple-element.7.gated_ref, f32[8,128]{1,0:T(8,128)S(1)} %get-tuple-element.8.scale_ref, f32[1,640]{1,0:T(1,128)S(1)} %reshape.11.gain_ref), custom_call_target="tpu_custom_call" | custom-call | tf_op jit(solution)/shard_map/norm/pallas_call | solution.py:543
  (5 shorter events, 0.0 us)
Async XLA Ops:
  0.0 4.3 %copy-start = (f32[4,640]{1,0:T(4,128)S(1)}, f32[4,640]{1,0:T(4,128)}, u32[]{:S(2)}) copy-start(f32[4,640]{1,0:T(4,128)} %conv_ref.1) | copy-start | bytes 30724

commit v2 on v1

--- a/solution.py
+++ b/solution.py
@@ -36,13 +36,14 @@
 
 
 def mixer_kernel(
-    hidden_ref, value_ref, gate_ref, small_ref, conv_ref, bc_conv_ref,
-    bias_ref, rate_ref, expand_ref,
+    hidden_ref, value_ref, gate_ref, bc_in, step_in, conv_in, bc_conv_in,
+    bias_in, rate_in, gain_in,
     gated_ref, scale_ref,
-    rows, weights, small_pre, bc_wide, fin, fout, ends, logs, pair_logs, chip_logs,
+    small_ref, step_cols, conv_ref, bc_taps, bc_square, bc_conv_ref,
+    bias_small, rate_small, bias_ref, rate_ref, gain_ref, expand_ref, rows, weights, small_pre, bc_wide, fin, fout, ends, logs, pair_logs, chip_logs,
     all_logs, early, late, pre, gates, scaled, right, other,
     local, pair, sent, got, prefix, owned, owned_pair, entering, sums, others,
-    load_sem, halo_sem, log_sem, log_send, log_recv, early_send, early_recv,
+    load_sem, small_sem, halo_sem, log_sem, log_send, log_recv, early_send, early_recv,
     late_send, late_recv, pair_sem, out_send, out_recv, back_send, back_recv,
     swap_sem, sum_send, sum_recv,
 ):
@@ -78,6 +79,16 @@
             device_id=device, device_id_type=MESH,
         )
 
+    little = [
+        pltpu.make_async_copy(source, target, small_sem.at[i])
+        for i, (source, target) in enumerate((
+            (bc_in, small_ref.at[pl.ds(narrow, narrow)]), (step_in, step_cols),
+            (bc_conv_in, bc_taps), (bias_in, bias_small), (rate_in, rate_small),
+            (conv_in, conv_ref), (gain_in, gain_ref),
+        ))
+    ]
+    for load in little:
+        load.start()
     chunk = length // 2
     loads = []
     for b in range(batch):
@@ -112,6 +123,24 @@
     for b in range(batch):
         rows[b, 0:HALO, :] = jnp.zeros((HALO, rows.shape[2]), BF16)
         small_pre[b, 0:LANES, :] = jnp.zeros((LANES, LANES), F32)
+    heads = step_cols.shape[0]
+    small_ref[0:narrow, :] = jnp.zeros((narrow, small_ref.shape[1]), BF16)
+    small_ref[2 * narrow :, :] = jnp.zeros((LANES - 2 * narrow, small_ref.shape[1]), BF16)
+    bias_ref[...] = jnp.zeros_like(bias_ref)
+    rate_ref[...] = jnp.zeros_like(rate_ref)
+    bc_square[...] = jnp.zeros_like(bc_square)
+    lane = lax.broadcasted_iota(jnp.int32, expand_ref.shape, 1) // HEAD_DIM
+    owner = lax.rem(lax.broadcasted_iota(jnp.int32, expand_ref.shape, 0), LANES)
+    expand_ref[...] = jnp.where(lane == owner, 1.0, 0.0).astype(BF16)
+    for load in little:
+        load.wait()
+    small_ref[0:heads, :] = step_cols[...]
+    bias_ref[:, 0:heads] = bias_small[...]
+    rate_ref[:, 0:heads] = jnp.exp(rate_small[...])
+    for part in range(2):
+        cut = slice(part * LANES, (part + 1) * LANES)
+        bc_square[0:CONV, :] = bc_taps[:, cut]
+        bc_conv_ref[cut, :] = jnp.transpose(bc_square[...])
     for b in range(batch):
         for part in range(2):
             loads[2 * b + part].wait()
@@ -137,7 +166,7 @@
 
     def transpose_bc(b, piece):
         at = slice(piece * LANES, (piece + 1) * LANES)
-        flipped = jnp.transpose(small_pre[b, at, :])[0:narrow, :]
+        flipped = jnp.transpose(small_pre[b, at, :])[narrow : 2 * narrow, :]
         bc_wide[b, :, at] = flipped.astype(BF16).astype(F32)
 
     for b in range(batch):
@@ -410,7 +439,7 @@
             for start in range(0, width, LANES):
                 cut = slice(start, start + LANES)
                 gated = gated_ref[b, at, cut] + other[b, at, cut] * extra[:, cut]
-                gated_ref[b, at, cut] = gated
+                gated_ref[b, at, cut] = gated * gain_ref[start // LANES : start // LANES + 1, :]
                 total = total + gated * gated
             sums[g : g + 1, :] = jnp.sum(jnp.transpose(total), axis=0, keepdims=True)
 
@@ -430,7 +459,7 @@
     scale_ref[...] = lax.rsqrt(whole_sq / DI + epsilon)
 
 
-def norm_kernel(gated_ref, scale_ref, gain_ref, out_ref):
+def norm_kernel(gated_ref, scale_ref, out_ref):
     width = gated_ref.shape[2]
     step = pl.program_id(0)
     count = gated_ref.shape[1] // BLOCK
@@ -440,9 +469,7 @@
         column = jnp.transpose(jnp.broadcast_to(line, (BLOCK, LANES)))
         for start in range(0, width, LANES):
             cut = slice(start, start + LANES)
-            out_ref[0, at, cut] = (
-                gated_ref[0, at, cut] * column * gain_ref[:, cut]
-            ).astype(BF16)
+            out_ref[0, at, cut] = (gated_ref[0, at, cut] * column).astype(BF16)
 
 
 def per_device(
@@ -462,16 +489,6 @@
     late_len = BLOCK
     early_len = length - late_len
 
-    tail = LANES - narrow - heads
-    small = jnp.concatenate(
-        [bc_proj.T, step_proj.T, jnp.zeros((tail, model_width), BF16)], axis=0
-    )
-    bias = jnp.pad(step_bias, (narrow, tail)).reshape(1, LANES)
-    rate = jnp.pad(jnp.exp(log_rate), (narrow, tail)).reshape(1, LANES)
-    lanes = lax.broadcasted_iota(jnp.int32, (2 * LANES, width), 1) // HEAD_DIM
-    owner = lax.broadcasted_iota(jnp.int32, (2 * LANES, width), 0) % LANES - narrow
-    expand = (lanes == owner).astype(BF16)
-
     hbm = pl.BlockSpec(memory_space=pltpu.HBM)
     vmem = pl.BlockSpec(memory_space=pltpu.VMEM)
     dma = pltpu.SemaphoreType.DMA
@@ -481,9 +498,21 @@
             jax.ShapeDtypeStruct((batch, length, width), F32),
             jax.ShapeDtypeStruct((total_blocks, LANES), F32),
         ),
-        in_specs=[hbm] * 3 + [vmem] * 6,
+        in_specs=[hbm] * 10,
         out_specs=[vmem, vmem],
         scratch_shapes=[
+            pltpu.VMEM((LANES, model_width), BF16),
+            pltpu.VMEM((heads, model_width), BF16),
+            pltpu.VMEM((CONV, width), F32),
+            pltpu.VMEM((CONV, 2 * STATE), F32),
+            pltpu.VMEM((LANES, LANES), F32),
+            pltpu.VMEM((2 * STATE, LANES), F32),
+            pltpu.VMEM((1, heads), F32),
+            pltpu.VMEM((1, heads), F32),
+            pltpu.VMEM((1, LANES), F32),
+            pltpu.VMEM((1, LANES), F32),
+            pltpu.VMEM((width // LANES, LANES), F32),
+            pltpu.VMEM((2 * LANES, width), BF16),
             pltpu.VMEM((batch, PAD + length, model_width), BF16),
             pltpu.VMEM((model_width, 2 * width), BF16),
             pltpu.VMEM((batch, LANES + length, LANES), F32),
@@ -513,6 +542,7 @@
             pltpu.VMEM((total_blocks, LANES), F32),
             pltpu.VMEM((tp - 1, total_blocks, LANES), F32),
             dma((2 * batch + 2,)),
+            dma((7,)),
             dma((2,)),
             dma((2,)),
             dma((chips - 1,)),
@@ -534,9 +564,11 @@
             vmem_limit_bytes=48 << 20, collective_id=0, has_side_effects=True
         ),
         name="mixer",
-    )(
-        hidden_in, value_proj, gate_proj, small, value_conv, bc_conv.T, bias, rate, expand,
-    )
+    )(*(pltpu.with_memory_space_constraint(x, pltpu.HBM) for x in (
+        hidden_in, value_proj, gate_proj, bc_proj.T, step_proj.T, value_conv, bc_conv,
+        step_bias.reshape(1, heads), log_rate.reshape(1, heads),
+        norm_gain.reshape(width // LANES, LANES),
+    )))
 
     part = 2 * BLOCK
     steps = length // part
@@ -547,12 +579,11 @@
         in_specs=[
             pl.BlockSpec((1, part, width), lambda s: (s // steps, s % steps, 0)),
             pl.BlockSpec((total_blocks, LANES), lambda s: (0, 0)),
-            pl.BlockSpec((1, width), lambda s: (0, 0)),
         ],
         out_specs=pl.BlockSpec((1, part, width), lambda s: (s // steps, s % steps, 0)),
         compiler_params=pltpu.CompilerParams(vmem_limit_bytes=12 << 20),
         name="norm",
-    )(gated, scale, norm_gain.reshape(1, width))
+    )(gated, scale)
 
 
 def solution(mesh):

time: 57.7 us -> 55.2 us (0.957)
  local copies, waits for them, and re-layouts: 2.99 us -> 0 us
  Pallas kernels: 53.1 us -> 55.1 us
  other arithmetic: 1.28 us -> 0 us
    pallas_call x1, Pallas kernels: 51.2 us -> 53.2 us  [per_device(): pl.pallas_call(mixer_kernel, out_shape=(jax.ShapeDtypeStruct((batch, leng...]
    reshape x2 -> x0, local copies, waits for them, and re-layouts: 1.42 us -> none  [the longest x1 0.73 us: per_device(): rate = jnp.pad(jnp.exp(log_rate), (narrow, tail)).reshape(1, LANES)]
    concatenate x1 -> x0, other arithmetic: 1.09 us -> none  [per_device(): jnp.concatenate([bc_proj.T, step_proj.T, jnp.zeros((tail, model_width), B...]
    unnamed x3 -> x0, local copies, waits for them, and re-layouts: 0.82 us -> none
    exp x1 -> x0, local copies, waits for them, and re-layouts: 0.67 us -> none  [per_device(): rate = jnp.pad(jnp.exp(log_rate), (narrow, tail)).reshape(1, LANES)]
where the time goes in v2:
time: 55.2 us; the launch traced here: 55.1 us
  Pallas kernels  55.1 us (100%)
    pallas_call x1, Pallas kernels, per_device(): pl.pallas_call(mixer_kernel, out_shape=(jax.ShapeDtypeStruct((batch, leng...  53.2 us
    pallas_call x1, Pallas kernels, per_device(): pl.pallas_call(norm_kernel, grid=(batch * steps,), out_shape=jax.ShapeDty...  1.88 us

profile of v2, /device:TPU:1, one launch (start us, length us, event | category | flops | bytes accessed | tf_op | source)
XLA Modules:
  0.0 55.1 jit_solution(13264916301068739495)
XLA Ops:
  0.0 53.2 %mixer.1 = (f32[2,512,640]{2,1,0:T(8,128)S(1)}, f32[8,128]{1,0:T(8,128)S(1)}) custom-call(bf16[2,512,2560]{2,1,0:T(8,128)(2,1)} %hidden_ref.1, bf16[2560,640]{1,0:T(8,128)(2,1)} %value_ref.1, bf16[2560,640]{1,0:T(8,128)(2,1)} %gate_ref.1, bf16[32,2560]{1,0:T(8,128)(2,1)} %bitcast.5, bf16[10,2560]{1,0:T(8,128)(2,1)} %bitcast.6, f32[4,640]{1,0:T(4,128)} %conv_in.1, ...), custom_call_target="tpu_custom_call" | custom-call | tf_op jit(solution)/shard_map/mixer/pallas_call | solution.py:495
  53.3 1.9 %norm.1 = bf16[2,512,640]{2,1,0:T(8,128)(2,1)} custom-call(f32[2,512,640]{2,1,0:T(8,128)S(1)} %get-tuple-element.7.gated_ref, f32[8,128]{1,0:T(8,128)S(1)} %get-tuple-element.8.scale_ref), custom_call_target="tpu_custom_call" | custom-call | tf_op jit(solution)/shard_map/norm/pallas_call | solution.py:575

commit v3 on v2

v3 whole, which is shorter than its diff:
```python
import jax
import jax.numpy as jnp
from jax import lax
from jax.experimental import pallas as pl
from jax.experimental.pallas import tpu as pltpu
from jax.sharding import PartitionSpec as P

DI = 5120
HEAD_DIM = 64
STATE = 128
CONV = 4
BLOCK = 128
LANES = 128
PAD = 16
HALO = 8
TILE = 256
SIDE = 4
MESH = pl.DeviceIdType.MESH

epsilon = 1e-05
F32 = jnp.float32
BF16 = jnp.bfloat16


def silu(x):
    return x * (1.0 / (1.0 + jnp.exp(-x)))


def halves(x):
    high = x.astype(BF16)
    low = (x - high.astype(F32)).astype(BF16)
    return jnp.concatenate([high, low], axis=1)


def dot_nt(a, b):
    return lax.dot_general(a, b, (((1,), (1,)), ((), ())), preferred_element_type=F32)


def mixer_kernel(
    hidden_ref, value_ref, gate_ref, bc_in, step_in, conv_in, bc_conv_in,
    bias_in, rate_in, gain_in,
    gated_ref, scale_ref,
    small_ref, step_cols, conv_ref, bc_taps, bc_square, bc_conv_ref,
    bias_small, rate_small, bias_ref, rate_ref, gain_ref, expand_ref, rows, weights, small_pre, bc_wide, fin, fout, ends, logs, pair_logs, chip_logs,
    all_logs, far, near, first_slots, pre, gates, left, right, other,
    local, pair, sent, got, prefix, owned, owned_pair, entering, sums, others,
    load_sem, small_sem, halo_sem, log_sem, log_send, log_recv, ring_send,
    far_recv, near_recv, first_recv, pair_sem, out_send, out_recv, back_send, back_recv,
    swap_sem, sum_send, sum_recv,
):
    batch, length, _ = hidden_ref.shape
    width = value_ref.shape[1]
    blocks = length // BLOCK
    total_blocks = batch * blocks
    narrow = bc_in.shape[0]
    me = lax.axis_index("tp")
    ring = lax.axis_size("tp")
    place = lax.axis_index("seq")
    devices = lax.axis_size("seq")
    chips = devices // 2
    core = lax.rem(place, 2)
    chip = place // 2
    partner = place + 1 - 2 * core
    after = lax.rem(place + 1, devices)
    before = lax.rem(place + devices - 1, devices)
    half = STATE // 2
    mine = pl.ds(pl.multiple_of(core * half, half), half)

    across = SIDE
    along = chips // SIDE

    def chip_at(move):
        dy, dx = move
        return (
            lax.rem(chip // across + dy, along) * across
            + lax.rem(lax.rem(chip, across) + dx, across)
        )

    def hops(away, count):
        return min(away, count - away)

    moves = sorted(
        [(dy, dx) for dy in range(along) for dx in range(across) if dy or dx],
        key=lambda move: -(hops(move[0], along) + hops(move[1], across)),
    )
    turns = sorted(range(1, lax.axis_size("tp")), key=lambda away: -hops(away, lax.axis_size("tp")))

    def wait_bytes(ref, count, semaphore):
        part = ref.at[pl.ds(0, count)]
        pltpu.make_async_copy(part, part, semaphore).wait()

    def tp_at(away):
        return lax.rem(me + away, ring)

    def remote(source, target, send, recv, **device):
        return pltpu.make_async_remote_copy(
            src_ref=source, dst_ref=target, send_sem=send, recv_sem=recv,
            device_id=device, device_id_type=MESH,
        )

    little = [
        pltpu.make_async_copy(source, target, small_sem.at[i])
        for i, (source, target) in enumerate((
            (bc_in, small_ref.at[pl.ds(narrow, narrow)]), (step_in, step_cols),
            (bc_conv_in, bc_taps), (bias_in, bias_small), (rate_in, rate_small),
            (conv_in, conv_ref), (gain_in, gain_ref),
        ))
    ]
    for load in little:
        load.start()
    chunk = length // 2
    loads = []
    for b in range(batch):
        for part in range(2):
            loads.append(pltpu.make_async_copy(
                hidden_ref.at[b, pl.ds(part * chunk, chunk)],
                rows.at[b, pl.ds(PAD + part * chunk, chunk)], load_sem.at[2 * b + part],
            ))
    gate_load = pltpu.make_async_copy(
        gate_ref, weights.at[:, pl.ds(width, width)], load_sem.at[2 * batch]
    )
    value_load = pltpu.make_async_copy(
        value_ref, weights.at[:, pl.ds(0, width)], load_sem.at[2 * batch + 1]
    )
    order = [2 * b + part for part in (1, 0) for b in range(batch)]
    for i in order:
        loads[i].start()

    barrier = pltpu.get_barrier_semaphore()
    for device in (after, before, partner):
        pl.semaphore_signal(barrier, inc=1, device_id={"seq": device}, device_id_type=MESH)
    for away in range(1, ring):
        pl.semaphore_signal(
            barrier, inc=1, device_id={"tp": tp_at(away)}, device_id_type=MESH
        )
    for move in moves:
        pl.semaphore_signal(
            barrier, inc=1, device_id={"seq": 2 * chip_at(move) + core}, device_id_type=MESH
        )

    for b in range(batch):
        rows[b, 0:HALO, :] = jnp.zeros((HALO, rows.shape[2]), BF16)
        small_pre[b, 0:LANES, :] = jnp.zeros((LANES, LANES), F32)
    heads = step_cols.shape[0]
    small_ref[0:narrow, :] = jnp.zeros((narrow, small_ref.shape[1]), BF16)
    small_ref[2 * narrow :, :] = jnp.zeros((LANES - 2 * narrow, small_ref.shape[1]), BF16)
    bias_ref[...] = jnp.zeros_like(bias_ref)
    rate_ref[...] = jnp.zeros_like(rate_ref)
    bc_square[...] = jnp.zeros_like(bc_square)
    lane = lax.broadcasted_iota(jnp.int32, expand_ref.shape, 1) // HEAD_DIM
    owner = lax.rem(lax.broadcasted_iota(jnp.int32, expand_ref.shape, 0), LANES)
    expand_ref[...] = jnp.where(lane == owner, 1.0, 0.0).astype(BF16)
    for load in little[:2]:
        load.wait()
    small_ref[0:heads, :] = step_cols[...]

    def small_product(part, b):
        loads[2 * b + part].wait()
        start = part * chunk
        small_pre[b, LANES + start : LANES + start + chunk, :] = dot_nt(
            rows[b, PAD + start : PAD + start + chunk, :], small_ref[...]
        )

    for b in range(batch):
        small_product(1, b)
    pl.semaphore_wait(barrier, 3 + (ring - 1) + (chips - 1))
    halo = remote(
        rows.at[:, pl.ds(PAD + length - HALO, HALO)], rows.at[:, pl.ds(PAD - HALO, HALO)],
        halo_sem.at[0], halo_sem.at[1], seq=after,
    )
    halo.start()
    value_load.start()
    for b in range(batch):
        small_product(0, b)
    for load in little[2:]:
        load.wait()
    bias_ref[:, 0:heads] = bias_small[...]
    rate_ref[:, 0:heads] = jnp.exp(rate_small[...])
    for part in range(2):
        cut = slice(part * LANES, (part + 1) * LANES)
        bc_square[0:CONV, :] = bc_taps[:, cut]
        bc_conv_ref[cut, :] = jnp.transpose(bc_square[...])
    taps = bc_conv_ref[pl.ds(pl.multiple_of(me * narrow, narrow), narrow), :]

    def bc_conv(x):
        total = taps[:, CONV - 1 : CONV] * x
        for k in range(1, CONV):
            total = total + taps[:, CONV - 1 - k : CONV - k] * pltpu.roll(x, k, 1)
        return silu(total).astype(BF16)

    def transpose_bc(b, piece):
        at = slice(piece * LANES, (piece + 1) * LANES)
        flipped = jnp.transpose(small_pre[b, at, :])[narrow : 2 * narrow, :]
        bc_wide[b, :, at] = flipped.astype(BF16).astype(F32)

    chunks = (
        (far, far_recv, blocks // 2, blocks, 1),
        (near, near_recv, 1, blocks // 2, -1),
        (first_slots, first_recv, 0, 1, -1),
    )

    def convolve(which):
        slots, _, low, high, _ = chunks[which]
        size = (high - low) * BLOCK
        for b in range(batch):
            done = bc_conv(bc_wide[b, :, low * LANES : (high + 1) * LANES])
            slots[me, :, b * size : (b + 1) * size] = done[:, LANES:]

    def ring_copy(which, source, steps, arrival):
        slots, recv = chunks[which][:2]
        source = tp_at(source % ring)
        return remote(
            slots.at[source], slots.at[source], ring_send.at[which], recv.at[arrival],
            tp=tp_at(steps % ring),
        )

    def ring_two(which):
        for way in (1, -1):
            ring_copy(which, 0, 2 * way, 0 if way == 1 else 1).start()

    def ring_one(which):
        for way in (1, -1):
            ring_copy(which, 0, way, 2).start()

    def ring_relay(which):
        for way in (1, -1):
            ring_copy(which, 0, 2 * way, 0 if way == 1 else 1).wait_recv()
            if chunks[which][4] == way:
                ring_copy(which, -2 * way, 2 * way, 2).start()
            ring_copy(which, -2 * way, way, 2).start()

    def ring_finish(which):
        slots, recv = chunks[which][:2]
        wait_bytes(slots, ring - 3, recv.at[2])

    def ring_sent(which):
        wait_bytes(chunks[which][0], ring - 1, ring_send.at[which])

    for b in range(batch):
        for piece in range(1, 1 + length // LANES):
            transpose_bc(b, piece)
    for which in range(2):
        convolve(which)
        ring_two(which)

    halo.wait()

    @pl.when(place == 0)
    def _():
        for b in range(batch):
            rows[b, 0:PAD, :] = jnp.zeros((PAD, rows.shape[2]), BF16)

    for b in range(batch):
        small_pre[b, LANES - PAD : LANES, :] = dot_nt(rows[b, 0:PAD, :], small_ref[...])
        transpose_bc(b, 0)
    convolve(2)
    ring_two(2)
    for which in range(3):
        ring_one(which)

    def gate_part(b, product):
        return silu(product.astype(BF16).astype(F32))

    def tile_of(index):
        cut = slice(index * TILE, (index + 1) * TILE)

        @pl.loop(0, batch)
        def _(b):
            if cut.start >= width:
                product = jnp.dot(
                    rows[b, PAD : PAD + length, :], weights[:, cut], preferred_element_type=F32
                )
                gates[b, :, cut.start - width : cut.stop - width] = gate_part(b, product)
            else:
                product = jnp.dot(rows[b], weights[:, cut], preferred_element_type=F32)
                inner = min(TILE, width - cut.start)
                pre[b, :, cut.start : cut.start + inner] = (
                    product[:, :inner].astype(BF16).astype(F32)
                )
                if inner < TILE:
                    gates[b, :, 0 : TILE - inner] = gate_part(b, product[PAD:, inner:])

    tiles = 2 * width // TILE
    value_tiles = -(-width // TILE)
    gate_load.start()
    value_load.wait()
    tile_of(0)

    row = lax.broadcasted_iota(jnp.int32, (BLOCK, BLOCK), 0)
    col = lax.broadcasted_iota(jnp.int32, (BLOCK, BLOCK), 1)
    triangle = jnp.where(row >= col, 1.0, 0.0).astype(F32)
    ms, mos, totals = [], [], []
    for b in range(batch):
        offset = jnp.zeros((1, LANES), F32)
        for k in range(blocks):
            step_pre = small_pre[b, LANES + k * BLOCK : LANES + (k + 1) * BLOCK, :] + bias_ref[...]
            steps = jnp.maximum(step_pre, 0.0) + jnp.log1p(jnp.exp(-jnp.abs(step_pre)))
            cumulative = jnp.dot(
                triangle, -steps * rate_ref[...],
                precision=lax.Precision.HIGHEST, preferred_element_type=F32,
            )
            last = cumulative[BLOCK - 1 : BLOCK, :]
            mid = 0.5 * last
            fin[b * blocks + k] = halves(jnp.exp(mid - cumulative) * steps)
            fout[b * blocks + k] = halves(jnp.exp(cumulative - mid))
            ms.append(mid)
            mos.append(mid + offset)
            offset = offset + last
        totals.append(offset)
    table = jnp.exp(jnp.concatenate(ms + mos, axis=0))
    ends[...] = jnp.dot(halves(table), expand_ref[...], preferred_element_type=F32)
    logs[...] = jnp.concatenate(totals + [jnp.zeros((8 - batch, LANES), F32)], axis=0)
    pair_log = remote(logs, pair_logs, log_sem.at[0], log_sem.at[1], seq=partner)
    pair_log.start()

    tile_of(1)
    for which in range(3):
        ring_relay(which)

    pair_log.wait()
    chip_logs[...] = logs[...] + pair_logs[...]
    all_logs[chip] = logs[...] + pair_logs[...]
    for move in moves:
        remote(
            chip_logs, all_logs.at[chip], log_send.at[0], log_recv.at[0],
            seq=2 * chip_at(move) + core,
        ).start()

    gate_load.wait()
    tile_of(2)

    def values_of(g):
        b, k = divmod(g, blocks)
        base = PAD + k * BLOCK - CONV + 1
        wide = jnp.dot(fin[g], expand_ref[...], preferred_element_type=F32)
        for start in range(0, width, LANES):
            cut = slice(start, start + LANES)
            x = conv_ref[0:1, cut] * pre[b, base : base + BLOCK, cut]
            for tap in range(1, CONV):
                x = x + conv_ref[tap : tap + 1, cut] * pre[
                    b, base + tap : base + tap + BLOCK, cut
                ]
            right[g, STATE:, cut] = (silu(x) * wide[:, cut]).astype(BF16)

    for g in range(total_blocks):
        values_of(g)
    for which in range(3):
        ring_finish(which)

    def bc_block(b, k, first):
        slots, _, low, high, _ = next(c for c in chunks if c[2] <= k < c[3])
        at = (b * (high - low) + k - low) * BLOCK
        return slots[first : first + ring // 2, :, at : at + BLOCK].reshape(STATE, BLOCK)

    for b in range(batch):
        held = jnp.zeros((STATE, width), F32)
        for k in range(blocks):
            g = b * blocks + k
            e = ends[g : g + 1, :]
            ahead = e * held
            right[g, :STATE, :] = ahead.astype(BF16)
            added = jnp.dot(
                bc_block(b, k, 0), right[g, STATE:, :], preferred_element_type=F32
            )
            held = e * (ahead + added)
        local[b] = held.astype(BF16)

    pair_copy = remote(local, pair, pair_sem.at[0], pair_sem.at[1], seq=partner)
    pair_copy.start()
    for g in range(total_blocks):
        b, k = divmod(g, blocks)
        b_flat = bc_block(b, k, 0)
        c_rows = jnp.transpose(bc_block(b, k, ring // 2).astype(F32)).astype(BF16)
        scores = jnp.dot(c_rows, b_flat, preferred_element_type=F32)
        left[g, :, :STATE] = c_rows
        left[g, :, STATE:] = jnp.where(row >= col, scores, 0.0).astype(BF16)
    wait_bytes(all_logs, chips - 1, log_send.at[0])
    wait_bytes(all_logs, chips - 1, log_recv.at[0])
    own_end = jnp.exp(logs[...])
    pair_end = jnp.exp(pair_logs[...])
    wide_ends = jnp.dot(
        halves(jnp.concatenate([own_end, pair_end], axis=0)), expand_ref[...],
        preferred_element_type=F32,
    )
    low = chip < chips // batch
    spans = jnp.concatenate(
        [jnp.where(low, all_logs[i, 0:1, :], all_logs[i, 1:2, :]) for i in range(chips)], axis=0
    )
    spans = jnp.dot(halves(jnp.exp(spans)), expand_ref[...], preferred_element_type=F32)

    pair_copy.wait()
    groups = chips // batch
    for b in range(batch):
        own = local[b, mine, :].astype(F32)
        theirs = pair[b, mine, :].astype(F32)
        first = jnp.where(core == 0, own, theirs)
        second = jnp.where(core == 0, theirs, own)
        later = jnp.where(core == 0, wide_ends[8 + b : 9 + b, :], wide_ends[b : b + 1, :])
        both = (later * first + second).reshape(groups, half // groups, width)
        sent[b * groups : (b + 1) * groups] = both.astype(BF16)
    got[chip] = sent[chip]
    for move in moves:
        peer = chip_at(move)
        remote(
            sent.at[peer], got.at[chip], out_send.at[0], out_recv.at[0], seq=2 * peer + core
        ).start()
    for index in range(value_tiles, tiles):
        tile_of(index)

    wait_bytes(got, chips - 1, out_send.at[0])
    wait_bytes(got, chips - 1, out_recv.at[0])
    running = jnp.zeros((half // groups, width), F32)
    for i in range(chips):
        prefix[i] = running.astype(BF16)
        if i + 1 < chips:
            running = spans[i : i + 1, :] * running + got[i].astype(F32)
    owned[chip] = prefix[chip]
    for move in moves:
        peer = chip_at(move)
        remote(
            prefix.at[peer], owned.at[chip], back_send.at[0], back_recv.at[0],
            seq=2 * peer + core,
        ).start()

    for g in range(total_blocks):
        b, k = divmod(g, blocks)
        at = slice(k * BLOCK, (k + 1) * BLOCK)
        wide = jnp.dot(fout[g], expand_ref[...], preferred_element_type=F32)
        y = jnp.dot(left[g], right[g], preferred_element_type=F32)
        weighted = wide * gates[b, at, :]
        gated_ref[b, at, :] = y * weighted
        other[b, at, :] = weighted * ends[total_blocks + g : total_blocks + g + 1, :]
    for which in range(3):
        ring_sent(which)
    wait_bytes(owned, chips - 1, back_send.at[0])
    wait_bytes(owned, chips - 1, back_recv.at[0])
    swap = remote(owned, owned_pair, swap_sem.at[0], swap_sem.at[1], seq=partner)
    swap.start()
    swap.wait()

    for b in range(batch):
        at = slice(b * groups, (b + 1) * groups)
        own = owned[at].astype(F32).reshape(half, width)
        theirs = owned_pair[at].astype(F32).reshape(half, width)
        span = wide_ends[8 + b : 9 + b, :]
        for c in range(2):
            cut = slice(c * half, (c + 1) * half)
            full = jnp.where(core == c, own, theirs)
            moved = span * full + pair[b, cut, :].astype(F32)
            entering[b, cut, :] = jnp.where(core == 0, full, moved).astype(BF16)

    for b in range(batch):
        for k in range(blocks):
            g = b * blocks + k
            at = slice(k * BLOCK, (k + 1) * BLOCK)
            extra = jnp.dot(left[g, :, :STATE], entering[b], preferred_element_type=F32)
            total = jnp.zeros((BLOCK, LANES), F32)
            for start in range(0, width, LANES):
                cut = slice(start, start + LANES)
                gated = gated_ref[b, at, cut] + other[b, at, cut] * extra[:, cut]
                gated_ref[b, at, cut] = gated * gain_ref[start // LANES : start // LANES + 1, :]
                total = total + gated * gated
            sums[g : g + 1, :] = jnp.sum(jnp.transpose(total), axis=0, keepdims=True)

    for away in turns:
        remote(sums, others.at[me], sum_send.at[0], sum_recv.at[0], tp=tp_at(away)).start()
    others[me] = sums[...]
    wait_bytes(others, ring - 1, sum_send.at[0])
    wait_bytes(others, ring - 1, sum_recv.at[0])
    whole_sq = others[0]
    for k in range(1, ring):
        whole_sq = whole_sq + others[k]
    scale_ref[...] = lax.rsqrt(whole_sq / DI + epsilon)


def norm_kernel(gated_ref, scale_ref, out_ref, done, sems):
    batch, length, width = gated_ref.shape
    copies = []
    for b in range(batch):
        for k in range(length // BLOCK):
            g = b * (length // BLOCK) + k
            at = slice(k * BLOCK, (k + 1) * BLOCK)
            column = jnp.transpose(jnp.broadcast_to(scale_ref[g : g + 1, :], (BLOCK, LANES)))
            for start in range(0, width, LANES):
                cut = slice(start, start + LANES)
                done[b, at, cut] = (gated_ref[b, at, cut] * column).astype(BF16)
            copies.append(pltpu.make_async_copy(
                done.at[b, pl.ds(k * BLOCK, BLOCK)], out_ref.at[b, pl.ds(k * BLOCK, BLOCK)],
                sems.at[g],
            ))
            copies[-1].start()
    for copy in copies:
        copy.wait()


def per_device(
    hidden_in, gate_proj, value_proj, bc_proj, step_proj,
    value_conv, bc_conv, step_bias, log_rate, norm_gain,
):
    batch, length, model_width = hidden_in.shape
    heads = step_proj.shape[1]
    width = value_proj.shape[1]
    narrow = bc_proj.shape[1]
    blocks = length // BLOCK
    tp = lax.axis_size("tp")
    chips = lax.axis_size("seq") // 2
    total_blocks = batch * blocks
    half = STATE // 2
    groups = chips // batch

    hbm = pl.BlockSpec(memory_space=pltpu.HBM)
    vmem = pl.BlockSpec(memory_space=pltpu.VMEM)
    dma = pltpu.SemaphoreType.DMA
    gated, scale = pl.pallas_call(
        mixer_kernel,
        out_shape=(
            jax.ShapeDtypeStruct((batch, length, width), F32),
            jax.ShapeDtypeStruct((total_blocks, LANES), F32),
        ),
        in_specs=[hbm] * 10,
        out_specs=[vmem, vmem],
        scratch_shapes=[
            pltpu.VMEM((LANES, model_width), BF16),
            pltpu.VMEM((heads, model_width), BF16),
            pltpu.VMEM((CONV, width), F32),
            pltpu.VMEM((CONV, 2 * STATE), F32),
            pltpu.VMEM((LANES, LANES), F32),
            pltpu.VMEM((2 * STATE, LANES), F32),
            pltpu.VMEM((1, heads), F32),
            pltpu.VMEM((1, heads), F32),
            pltpu.VMEM((1, LANES), F32),
            pltpu.VMEM((1, LANES), F32),
            pltpu.VMEM((width // LANES, LANES), F32),
            pltpu.VMEM((2 * LANES, width), BF16),
            pltpu.VMEM((batch, PAD + length, model_width), BF16),
            pltpu.VMEM((model_width, 2 * width), BF16),
            pltpu.VMEM((batch, LANES + length, LANES), F32),
            pltpu.VMEM((batch, narrow, LANES + length), F32),
            pltpu.VMEM((total_blocks, BLOCK, 2 * LANES), BF16),
            pltpu.VMEM((total_blocks, BLOCK, 2 * LANES), BF16),
            pltpu.VMEM((2 * total_blocks, width), F32),
            pltpu.VMEM((8, LANES), F32),
            pltpu.VMEM((8, LANES), F32),
            pltpu.VMEM((8, LANES), F32),
            pltpu.VMEM((chips, 8, LANES), F32),
            pltpu.VMEM((tp, narrow, batch * (blocks - blocks // 2) * BLOCK), BF16),
            pltpu.VMEM((tp, narrow, batch * (blocks // 2 - 1) * BLOCK), BF16),
            pltpu.VMEM((tp, narrow, batch * BLOCK), BF16),
            pltpu.VMEM((batch, PAD + length, width), F32),
            pltpu.VMEM((batch, length, width), F32),
            pltpu.VMEM((total_blocks, BLOCK, STATE + BLOCK), BF16),
            pltpu.VMEM((total_blocks, STATE + BLOCK, width), BF16),
            pltpu.VMEM((batch, length, width), F32),
            pltpu.VMEM((batch, STATE, width), BF16),
            pltpu.VMEM((batch, STATE, width), BF16),
            pltpu.VMEM((chips, half // groups, width), BF16),
            pltpu.VMEM((chips, half // groups, width), BF16),
            pltpu.VMEM((chips, half // groups, width), BF16),
            pltpu.VMEM((chips, half // groups, width), BF16),
            pltpu.VMEM((chips, half // groups, width), BF16),
            pltpu.VMEM((batch, STATE, width), BF16),
            pltpu.VMEM((total_blocks, LANES), F32),
            pltpu.VMEM((tp, total_blocks, LANES), F32),
            dma((2 * batch + 2,)),
            dma((7,)),
            dma((2,)),
            dma((2,)),
            dma((1,)),
            dma((1,)),
            dma((3,)),
            dma((3,)),
            dma((3,)),
            dma((3,)),
            dma((2,)),
            dma((1,)),
            dma((1,)),
            dma((1,)),
            dma((1,)),
            dma((2,)),
            dma((1,)),
            dma((1,)),
        ],
        compiler_params=pltpu.CompilerParams(
            vmem_limit_bytes=48 << 20, collective_id=0, has_side_effects=True
        ),
        name="mixer",
    )(*(pltpu.with_memory_space_constraint(x, pltpu.HBM) for x in (
        hidden_in, value_proj, gate_proj, bc_proj.T, step_proj.T, value_conv, bc_conv,
        step_bias.reshape(1, heads), log_rate.reshape(1, heads),
        norm_gain.reshape(width // LANES, LANES),
    )))

    return pl.pallas_call(
        norm_kernel,
        out_shape=jax.ShapeDtypeStruct((batch, length, width), BF16),
        in_specs=[vmem, vmem],
        out_specs=hbm,
        scratch_shapes=[pltpu.VMEM((batch, length, width), BF16), dma((total_blocks,))],
        compiler_params=pltpu.CompilerParams(vmem_limit_bytes=8 << 20),
        name="norm",
    )(gated, scale)


def solution(mesh):
    return jax.shard_map(
        per_device,
        mesh=mesh,
        in_specs=(
            P(None, "seq", None),
            P(None, "tp"),
            P(None, "tp"),
            P(None, "tp"),
            P(None, "tp"),
            P(None, "tp"),
            P(),
            P("tp"),
            P("tp"),
            P("tp"),
        ),
        out_specs=P(None, "seq", "tp"),
        check_vma=False,
    )
```

time: 55.2 us -> 44.9 us (0.81)
  Pallas kernels: 55.1 us -> 44.8 us
    pallas_call x1, Pallas kernels: 53.2 us -> 43.6 us  [per_device(): pl.pallas_call(mixer_kernel, out_shape=(jax.ShapeDtypeStruct((batch, leng...]
    pallas_call x1, Pallas kernels: 1.88 us -> 1.22 us  [per_device(): pl.pallas_call(norm_kernel, out_shape=jax.ShapeDtypeStruct((batch, length...]
where the time goes in v3:
time: 44.9 us; the launch traced here: 44.8 us
  Pallas kernels  44.8 us (100%)
    pallas_call x1, Pallas kernels, per_device(): pl.pallas_call(mixer_kernel, out_shape=(jax.ShapeDtypeStruct((batch, leng...  43.6 us
    pallas_call x1, Pallas kernels, per_device(): pl.pallas_call(norm_kernel, out_shape=jax.ShapeDtypeStruct((batch, length...  1.22 us

profile of v3, /device:TPU:1, one launch (start us, length us, event | category | flops | bytes accessed | tf_op | source)
XLA Modules:
  0.0 44.8 jit_solution(4134944409780774040)
XLA Ops:
  0.0 43.6 %mixer.1 = (f32[2,512,640]{2,1,0:T(8,128)S(1)}, f32[8,128]{1,0:T(8,128)S(1)}) custom-call(bf16[2,512,2560]{2,1,0:T(8,128)(2,1)} %hidden_ref.1, bf16[2560,640]{1,0:T(8,128)(2,1)} %value_ref.1, bf16[2560,640]{1,0:T(8,128)(2,1)} %gate_ref.1, bf16[32,2560]{1,0:T(8,128)(2,1)} %bitcast.5, bf16[10,2560]{1,0:T(8,128)(2,1)} %bitcast.6, f32[4,640]{1,0:T(4,128)} %conv_in.1, ...), custom_call_target="tpu_custom_call" | custom-call | tf_op jit(solution)/shard_map/mixer/pallas_call | solution.py:514
  43.6 1.2 %norm.1 = bf16[2,512,640]{2,1,0:T(8,128)(2,1)} custom-call(f32[2,512,640]{2,1,0:T(8,128)S(1)} %get-tuple-element.7.gated_ref, f32[8,128]{1,0:T(8,128)S(1)} %get-tuple-element.8.scale_ref), custom_call_target="tpu_custom_call" | custom-call | tf_op jit(solution)/shard_map/norm/pallas_call | solution.py:593

commit v4 on v3

--- a/solution.py
+++ b/solution.py
@@ -15,6 +15,7 @@
 HALO = 8
 TILE = 256
 SIDE = 4
+GREETED = (1, 2, 6, 7)
 MESH = pl.DeviceIdType.MESH
 
 epsilon = 1e-05
@@ -23,7 +24,8 @@
 
 
 def silu(x):
-    return x * (1.0 / (1.0 + jnp.exp(-x)))
+    halved = 0.5 * x
+    return halved + halved * jnp.tanh(halved)
 
 
 def halves(x):
@@ -32,15 +34,19 @@
     return jnp.concatenate([high, low], axis=1)
 
 
-def dot_nt(a, b):
-    return lax.dot_general(a, b, (((1,), (1,)), ((), ())), preferred_element_type=F32)
+def thirds(x):
+    terms = []
+    for _ in range(3):
+        terms.append(x.astype(BF16))
+        x = x - terms[-1].astype(F32)
+    return jnp.concatenate(terms, axis=0)
 
 
 def mixer_kernel(
     hidden_ref, value_ref, gate_ref, bc_in, step_in, conv_in, bc_conv_in,
     bias_in, rate_in, gain_in,
     gated_ref, scale_ref,
-    small_ref, step_cols, conv_ref, bc_taps, bc_square, bc_conv_ref,
+    small_ref, first_weights, step_cols, conv_ref, bc_taps, bc_square, bc_conv_ref,
     bias_small, rate_small, bias_ref, rate_ref, gain_ref, expand_ref, rows, weights, small_pre, bc_wide, fin, fout, ends, logs, pair_logs, chip_logs,
     all_logs, far, near, first_slots, pre, gates, left, right, other,
     local, pair, sent, got, prefix, owned, owned_pair, entering, sums, others,
@@ -65,6 +71,7 @@
     before = lax.rem(place + devices - 1, devices)
     half = STATE // 2
     mine = pl.ds(pl.multiple_of(core * half, half), half)
+    theirs_at = pl.ds(pl.multiple_of(half - core * half, half), half)
 
     across = SIDE
     along = chips // SIDE
@@ -116,12 +123,19 @@
                 hidden_ref.at[b, pl.ds(part * chunk, chunk)],
                 rows.at[b, pl.ds(PAD + part * chunk, chunk)], load_sem.at[2 * b + part],
             ))
+    body = width - LANES
     gate_load = pltpu.make_async_copy(
-        gate_ref, weights.at[:, pl.ds(width, width)], load_sem.at[2 * batch]
+        gate_ref, weights.at[:, pl.ds(body, width)], load_sem.at[2 * batch]
     )
     value_load = pltpu.make_async_copy(
-        value_ref, weights.at[:, pl.ds(0, width)], load_sem.at[2 * batch + 1]
-    )
+        value_ref.at[:, pl.ds(0, body)], weights.at[:, pl.ds(0, body)],
+        load_sem.at[2 * batch + 1],
+    )
+    tail_load = pltpu.make_async_copy(
+        value_ref.at[:, pl.ds(body, LANES)], first_weights.at[:, pl.ds(LANES, LANES)],
+        load_sem.at[2 * batch + 2],
+    )
+    tail_load.start()
     order = [2 * b + part for part in (1, 0) for b in range(batch)]
     for i in order:
         loads[i].start()
@@ -129,7 +143,7 @@
     barrier = pltpu.get_barrier_semaphore()
     for device in (after, before, partner):
         pl.semaphore_signal(barrier, inc=1, device_id={"seq": device}, device_id_type=MESH)
-    for away in range(1, ring):
+    for away in GREETED:
         pl.semaphore_signal(
             barrier, inc=1, device_id={"tp": tp_at(away)}, device_id_type=MESH
         )
@@ -154,24 +168,39 @@
         load.wait()
     small_ref[0:heads, :] = step_cols[...]
 
-    def small_product(part, b):
-        loads[2 * b + part].wait()
-        start = part * chunk
-        small_pre[b, LANES + start : LANES + start + chunk, :] = dot_nt(
-            rows[b, PAD + start : PAD + start + chunk, :], small_ref[...]
-        )
-
-    for b in range(batch):
-        small_product(1, b)
-    pl.semaphore_wait(barrier, 3 + (ring - 1) + (chips - 1))
+    for at in range(0, small_ref.shape[1], LANES):
+        first_weights[at : at + LANES, :LANES] = jnp.transpose(small_ref[:, at : at + LANES])
+
+    def first_products(product, b, small_at, value_at):
+        small_pre[b, small_at, :] = product[:, :LANES]
+        pre[b, value_at, body:] = product[:, LANES:].astype(BF16).astype(F32)
+
+    tail_load.wait()
+
+    @pl.loop(0, 2 * batch)
+    def _(i):
+        part = 1 - i // batch
+        b = lax.rem(i, batch)
+        start = pl.multiple_of(part * chunk, chunk)
+        pltpu.make_async_copy(
+            hidden_ref.at[b, pl.ds(start, chunk)], rows.at[b, pl.ds(PAD + start, chunk)],
+            load_sem.at[2 * b + part],
+        ).wait()
+        product = jnp.dot(
+            rows[b, pl.ds(PAD + start, chunk), :], first_weights[...], preferred_element_type=F32
+        )
+        first_products(product, b, pl.ds(LANES + start, chunk), pl.ds(PAD + start, chunk))
+
+    pl.semaphore_wait(barrier, 3 + len(GREETED) + (chips - 1))
     halo = remote(
         rows.at[:, pl.ds(PAD + length - HALO, HALO)], rows.at[:, pl.ds(PAD - HALO, HALO)],
         halo_sem.at[0], halo_sem.at[1], seq=after,
     )
-    halo.start()
+    @pl.when(place < devices - 1)
+    def _():
+        halo.start()
+
     value_load.start()
-    for b in range(batch):
-        small_product(0, b)
     for load in little[2:]:
         load.wait()
     bias_ref[:, 0:heads] = bias_small[...]
@@ -198,6 +227,7 @@
         (near, near_recv, 1, blocks // 2, -1),
         (first_slots, first_recv, 0, 1, -1),
     )
+    b_way = jnp.where(jnp.logical_and(me >= 2, me < 2 + ring // 2), 1, -1)
 
     def convolve(which):
         slots, _, low, high, _ = chunks[which]
@@ -206,32 +236,32 @@
             done = bc_conv(bc_wide[b, :, low * LANES : (high + 1) * LANES])
             slots[me, :, b * size : (b + 1) * size] = done[:, LANES:]
 
-    def ring_copy(which, source, steps, arrival):
+    def ring_copy(which, source, target):
         slots, recv = chunks[which][:2]
-        source = tp_at(source % ring)
         return remote(
-            slots.at[source], slots.at[source], ring_send.at[which], recv.at[arrival],
-            tp=tp_at(steps % ring),
-        )
-
-    def ring_two(which):
-        for way in (1, -1):
-            ring_copy(which, 0, 2 * way, 0 if way == 1 else 1).start()
-
-    def ring_one(which):
-        for way in (1, -1):
-            ring_copy(which, 0, way, 2).start()
-
-    def ring_relay(which):
-        for way in (1, -1):
-            ring_copy(which, 0, 2 * way, 0 if way == 1 else 1).wait_recv()
-            if chunks[which][4] == way:
-                ring_copy(which, -2 * way, 2 * way, 2).start()
-            ring_copy(which, -2 * way, way, 2).start()
-
-    def ring_finish(which):
-        slots, recv = chunks[which][:2]
-        wait_bytes(slots, ring - 3, recv.at[2])
+            slots.at[source], slots.at[source], ring_send.at[which], recv.at[source], tp=target
+        )
+
+    def ring_own(which, steps):
+        for away in (steps, ring - steps):
+            ring_copy(which, me, tp_at(away)).start()
+
+    def ring_relay(which, way):
+        source = tp_at(ring - 2 * way)
+        ring_copy(which, source, tp_at(1)).wait_recv()
+
+        @pl.when(way == chunks[which][4])
+        def _():
+            ring_copy(which, source, tp_at(ring + 2 * way)).start()
+
+        ring_copy(which, source, tp_at(ring + way)).start()
+
+    def ring_finish(which, first, way):
+        passed = tp_at(ring - 2 * way)
+        for source in range(first, first + ring // 2):
+            @pl.when(jnp.logical_and(me != source, passed != source))
+            def _():
+                ring_copy(which, source, tp_at(1)).wait_recv()
 
     def ring_sent(which):
         wait_bytes(chunks[which][0], ring - 1, ring_send.at[which])
@@ -241,54 +271,14 @@
             transpose_bc(b, piece)
     for which in range(2):
         convolve(which)
-        ring_two(which)
-
-    halo.wait()
-
-    @pl.when(place == 0)
-    def _():
-        for b in range(batch):
-            rows[b, 0:PAD, :] = jnp.zeros((PAD, rows.shape[2]), BF16)
-
-    for b in range(batch):
-        small_pre[b, LANES - PAD : LANES, :] = dot_nt(rows[b, 0:PAD, :], small_ref[...])
-        transpose_bc(b, 0)
-    convolve(2)
-    ring_two(2)
-    for which in range(3):
-        ring_one(which)
-
-    def gate_part(b, product):
-        return silu(product.astype(BF16).astype(F32))
-
-    def tile_of(index):
-        cut = slice(index * TILE, (index + 1) * TILE)
-
-        @pl.loop(0, batch)
-        def _(b):
-            if cut.start >= width:
-                product = jnp.dot(
-                    rows[b, PAD : PAD + length, :], weights[:, cut], preferred_element_type=F32
-                )
-                gates[b, :, cut.start - width : cut.stop - width] = gate_part(b, product)
-            else:
-                product = jnp.dot(rows[b], weights[:, cut], preferred_element_type=F32)
-                inner = min(TILE, width - cut.start)
-                pre[b, :, cut.start : cut.start + inner] = (
-                    product[:, :inner].astype(BF16).astype(F32)
-                )
-                if inner < TILE:
-                    gates[b, :, 0 : TILE - inner] = gate_part(b, product[PAD:, inner:])
-
-    tiles = 2 * width // TILE
-    value_tiles = -(-width // TILE)
-    gate_load.start()
-    value_load.wait()
-    tile_of(0)
+        ring_own(which, 2)
+    for which in range(2):
+        ring_own(which, 1)
 
     row = lax.broadcasted_iota(jnp.int32, (BLOCK, BLOCK), 0)
     col = lax.broadcasted_iota(jnp.int32, (BLOCK, BLOCK), 1)
-    triangle = jnp.where(row >= col, 1.0, 0.0).astype(F32)
+    triangle = jnp.where(row >= col, 1.0, 0.0).astype(BF16)
+    triangle = jnp.concatenate([triangle] * 3, axis=1)
     ms, mos, totals = [], [], []
     for b in range(batch):
         offset = jnp.zeros((1, LANES), F32)
@@ -296,8 +286,7 @@
             step_pre = small_pre[b, LANES + k * BLOCK : LANES + (k + 1) * BLOCK, :] + bias_ref[...]
             steps = jnp.maximum(step_pre, 0.0) + jnp.log1p(jnp.exp(-jnp.abs(step_pre)))
             cumulative = jnp.dot(
-                triangle, -steps * rate_ref[...],
-                precision=lax.Precision.HIGHEST, preferred_element_type=F32,
+                triangle, thirds(-steps * rate_ref[...]), preferred_element_type=F32
             )
             last = cumulative[BLOCK - 1 : BLOCK, :]
             mid = 0.5 * last
@@ -313,9 +302,56 @@
     pair_log = remote(logs, pair_logs, log_sem.at[0], log_sem.at[1], seq=partner)
     pair_log.start()
 
-    tile_of(1)
-    for which in range(3):
-        ring_relay(which)
+    @pl.when(place < devices - 1)
+    def _():
+        halo.wait_send()
+
+    @pl.when(place > 0)
+    def _():
+        halo.wait_recv()
+
+    @pl.when(place == 0)
+    def _():
+        for b in range(batch):
+            rows[b, 0:PAD, :] = jnp.zeros((PAD, rows.shape[2]), BF16)
+
+    product = jnp.dot(
+        jnp.concatenate([rows[b, 0:PAD, :] for b in range(batch)], axis=0), first_weights[...],
+        preferred_element_type=F32,
+    )
+    for b in range(batch):
+        first_products(
+            product[b * PAD : (b + 1) * PAD], b, slice(LANES - PAD, LANES), slice(0, PAD)
+        )
+        transpose_bc(b, 0)
+    convolve(2)
+    ring_own(2, 2)
+    ring_own(2, 1)
+
+    def gate_part(b, product):
+        return silu(product.astype(BF16).astype(F32))
+
+    def tile_of(start, size):
+        cut = slice(start, start + size)
+
+        @pl.loop(0, batch)
+        def _(b):
+            if start >= body:
+                product = jnp.dot(
+                    rows[b, PAD : PAD + length, :], weights[:, cut], preferred_element_type=F32
+                )
+                gates[b, :, start - body : start - body + size] = gate_part(b, product)
+            else:
+                product = jnp.dot(rows[b], weights[:, cut], preferred_element_type=F32)
+                pre[b, :, cut] = product.astype(BF16).astype(F32)
+
+    value_tiles = [(at, TILE) for at in range(0, body, TILE)]
+    gate_tiles = [
+        (at, min(TILE, body + width - at)) for at in range(body, body + width, TILE)
+    ]
+    gate_load.start()
+    value_load.wait()
+    tile_of(*value_tiles[0])
 
     pair_log.wait()
     chip_logs[...] = logs[...] + pair_logs[...]
@@ -325,27 +361,28 @@
             chip_logs, all_logs.at[chip], log_send.at[0], log_recv.at[0],
             seq=2 * chip_at(move) + core,
         ).start()
-
-    gate_load.wait()
-    tile_of(2)
+    for which in range(2):
+        ring_relay(which, b_way)
+    for start, size in value_tiles[1:]:
+        tile_of(start, size)
+    ring_relay(2, b_way)
 
     def values_of(g):
         b, k = divmod(g, blocks)
-        base = PAD + k * BLOCK - CONV + 1
+        base = PAD + k * BLOCK - HALO
         wide = jnp.dot(fin[g], expand_ref[...], preferred_element_type=F32)
         for start in range(0, width, LANES):
             cut = slice(start, start + LANES)
-            x = conv_ref[0:1, cut] * pre[b, base : base + BLOCK, cut]
+            window = pre[b, base : base + HALO + BLOCK, cut]
+            x = conv_ref[0:1, cut] * window
             for tap in range(1, CONV):
-                x = x + conv_ref[tap : tap + 1, cut] * pre[
-                    b, base + tap : base + tap + BLOCK, cut
-                ]
-            right[g, STATE:, cut] = (silu(x) * wide[:, cut]).astype(BF16)
+                x = pltpu.roll(x, 1, 0) + conv_ref[tap : tap + 1, cut] * window
+            right[g, STATE:, cut] = (silu(x[HALO:]) * wide[:, cut]).astype(BF16)
 
     for g in range(total_blocks):
         values_of(g)
     for which in range(3):
-        ring_finish(which)
+        ring_finish(which, 0, b_way)
 
     def bc_block(b, k, first):
         slots, _, low, high, _ = next(c for c in chunks if c[2] <= k < c[3])
@@ -365,15 +402,16 @@
             held = e * (ahead + added)
         local[b] = held.astype(BF16)
 
-    pair_copy = remote(local, pair, pair_sem.at[0], pair_sem.at[1], seq=partner)
-    pair_copy.start()
-    for g in range(total_blocks):
-        b, k = divmod(g, blocks)
-        b_flat = bc_block(b, k, 0)
-        c_rows = jnp.transpose(bc_block(b, k, ring // 2).astype(F32)).astype(BF16)
-        scores = jnp.dot(c_rows, b_flat, preferred_element_type=F32)
-        left[g, :, :STATE] = c_rows
-        left[g, :, STATE:] = jnp.where(row >= col, scores, 0.0).astype(BF16)
+    def pair_copy(at, index):
+        return remote(
+            local.at[:, at], pair.at[:, at], pair_sem.at[index], pair_sem.at[index + 1],
+            seq=partner,
+        )
+
+    pair_copy(theirs_at, 0).start()
+    pair_copy(mine, 2).start()
+    for which in range(3):
+        ring_relay(which, -b_way)
     wait_bytes(all_logs, chips - 1, log_send.at[0])
     wait_bytes(all_logs, chips - 1, log_recv.at[0])
     own_end = jnp.exp(logs[...])
@@ -388,7 +426,7 @@
     )
     spans = jnp.dot(halves(jnp.exp(spans)), expand_ref[...], preferred_element_type=F32)
 
-    pair_copy.wait()
+    pair_copy(theirs_at, 0).wait()
     groups = chips // batch
     for b in range(batch):
         own = local[b, mine, :].astype(F32)
@@ -404,8 +442,9 @@
         remote(
             sent.at[peer], got.at[chip], out_send.at[0], out_recv.at[0], seq=2 * peer + core
         ).start()
-    for index in range(value_tiles, tiles):
-        tile_of(index)
+    gate_load.wait()
+    for start, size in gate_tiles[:2]:
+        tile_of(start, size)
 
     wait_bytes(got, chips - 1, out_send.at[0])
     wait_bytes(got, chips - 1, out_recv.at[0])
@@ -422,6 +461,17 @@
             seq=2 * peer + core,
         ).start()
 
+    for start, size in gate_tiles[2:]:
+        tile_of(start, size)
+    for which in range(3):
+        ring_finish(which, ring // 2, -b_way)
+    for g in range(total_blocks):
+        b, k = divmod(g, blocks)
+        b_flat = bc_block(b, k, 0)
+        c_rows = jnp.transpose(bc_block(b, k, ring // 2).astype(F32)).astype(BF16)
+        scores = jnp.dot(c_rows, b_flat, preferred_element_type=F32)
+        left[g, :, :STATE] = c_rows
+        left[g, :, STATE:] = jnp.where(row >= col, scores, 0.0).astype(BF16)
     for g in range(total_blocks):
         b, k = divmod(g, blocks)
         at = slice(k * BLOCK, (k + 1) * BLOCK)
@@ -436,6 +486,7 @@
     wait_bytes(owned, chips - 1, back_recv.at[0])
     swap = remote(owned, owned_pair, swap_sem.at[0], swap_sem.at[1], seq=partner)
     swap.start()
+    pair_copy(mine, 2).wait()
     swap.wait()
 
     for b in range(batch):
@@ -521,6 +572,7 @@
         out_specs=[vmem, vmem],
         scratch_shapes=[
             pltpu.VMEM((LANES, model_width), BF16),
+            pltpu.VMEM((model_width, 2 * LANES), BF16),
             pltpu.VMEM((heads, model_width), BF16),
             pltpu.VMEM((CONV, width), F32),
             pltpu.VMEM((CONV, 2 * STATE), F32),
@@ -533,7 +585,7 @@
             pltpu.VMEM((width // LANES, LANES), F32),
             pltpu.VMEM((2 * LANES, width), BF16),
             pltpu.VMEM((batch, PAD + length, model_width), BF16),
-            pltpu.VMEM((model_width, 2 * width), BF16),
+            pltpu.VMEM((model_width, 2 * width - LANES), BF16),
             pltpu.VMEM((batch, LANES + length, LANES), F32),
             pltpu.VMEM((batch, narrow, LANES + length), F32),
             pltpu.VMEM((total_blocks, BLOCK, 2 * LANES), BF16),
@@ -561,17 +613,17 @@
             pltpu.VMEM((batch, STATE, width), BF16),
             pltpu.VMEM((total_blocks, LANES), F32),
             pltpu.VMEM((tp, total_blocks, LANES), F32),
-            dma((2 * batch + 2,)),
+            dma((2 * batch + 3,)),
             dma((7,)),
             dma((2,)),
             dma((2,)),
             dma((1,)),
             dma((1,)),
             dma((3,)),
-            dma((3,)),
-            dma((3,)),
-            dma((3,)),
-            dma((2,)),
+            dma((tp,)),
+            dma((tp,)),
+            dma((tp,)),
+            dma((4,)),
             dma((1,)),
             dma((1,)),
             dma((1,)),

time: 44.9 us -> 41.5 us (0.924)
  Pallas kernels: 44.8 us -> 41.4 us
    pallas_call x1, Pallas kernels: 43.6 us -> 40.2 us  [per_device(): pl.pallas_call(mixer_kernel, out_shape=(jax.ShapeDtypeStruct((batch, leng...]
where the time goes in v4:
time: 41.5 us; the launch traced here: 41.4 us
  Pallas kernels  41.4 us (100%)
    pallas_call x1, Pallas kernels, per_device(): pl.pallas_call(mixer_kernel, out_shape=(jax.ShapeDtypeStruct((batch, leng...  40.2 us
    pallas_call x1, Pallas kernels, per_device(): pl.pallas_call(norm_kernel, out_shape=jax.ShapeDtypeStruct((batch, length...  1.22 us

profile of v4, /device:TPU:1, one launch (start us, length us, event | category | flops | bytes accessed | tf_op | source)
XLA Modules:
  0.0 41.4 jit_solution(382283064828924594)
XLA Ops:
  0.0 40.2 %mixer.1 = (f32[2,512,640]{2,1,0:T(8,128)S(1)}, f32[8,128]{1,0:T(8,128)S(1)}) custom-call(bf16[2,512,2560]{2,1,0:T(8,128)(2,1)} %hidden_ref.1, bf16[2560,640]{1,0:T(8,128)(2,1)} %value_ref.1, bf16[2560,640]{1,0:T(8,128)(2,1)} %gate_ref.1, bf16[32,2560]{1,0:T(8,128)(2,1)} %bitcast.5, bf16[10,2560]{1,0:T(8,128)(2,1)} %bitcast.6, f32[4,640]{1,0:T(4,128)} %conv_in.1, ...), custom_call_target="tpu_custom_call" | custom-call | tf_op jit(solution)/shard_map/mixer/pallas_call | solution.py:565
  40.2 1.2 %norm.1 = bf16[2,512,640]{2,1,0:T(8,128)(2,1)} custom-call(f32[2,512,640]{2,1,0:T(8,128)S(1)} %get-tuple-element.7.gated_ref, f32[8,128]{1,0:T(8,128)S(1)} %get-tuple-element.8.scale_ref), custom_call_target="tpu_custom_call" | custom-call | tf_op jit(solution)/shard_map/norm/pallas_call | solution.py:645

commit v5 on v4

--- a/solution.py
+++ b/solution.py
@@ -50,7 +50,7 @@
     bias_small, rate_small, bias_ref, rate_ref, gain_ref, expand_ref, rows, weights, small_pre, bc_wide, fin, fout, ends, logs, pair_logs, chip_logs,
     all_logs, far, near, first_slots, pre, gates, left, right, other,
     local, pair, sent, got, prefix, owned, owned_pair, entering, sums, others,
-    load_sem, small_sem, halo_sem, log_sem, log_send, log_recv, ring_send,
+    greet_sem, load_sem, small_sem, halo_sem, log_sem, log_send, log_recv, ring_send,
     far_recv, near_recv, first_recv, pair_sem, out_send, out_recv, back_send, back_recv,
     swap_sem, sum_send, sum_recv,
 ):
@@ -147,10 +147,20 @@
         pl.semaphore_signal(
             barrier, inc=1, device_id={"tp": tp_at(away)}, device_id_type=MESH
         )
-    for move in moves:
-        pl.semaphore_signal(
-            barrier, inc=1, device_id={"seq": 2 * chip_at(move) + core}, device_id_type=MESH
-        )
+    def greet(semaphore):
+        for move in ((0, 1), (0, across - 1), (1, 0), (along - 1, 0)):
+            pl.semaphore_signal(
+                semaphore, inc=1, device_id={"seq": 2 * chip_at(move) + core},
+                device_id_type=MESH,
+            )
+
+    greet(barrier)
+
+    def greet_round(index):
+        if index > 0:
+            pl.semaphore_wait(greet_sem.at[index - 1], 4)
+        if index < across // 2 + along // 2 - 1:
+            greet(greet_sem.at[index])
 
     for b in range(batch):
         rows[b, 0:HALO, :] = jnp.zeros((HALO, rows.shape[2]), BF16)
@@ -177,21 +187,23 @@
 
     tail_load.wait()
 
-    @pl.loop(0, 2 * batch)
-    def _(i):
-        part = 1 - i // batch
-        b = lax.rem(i, batch)
-        start = pl.multiple_of(part * chunk, chunk)
-        pltpu.make_async_copy(
-            hidden_ref.at[b, pl.ds(start, chunk)], rows.at[b, pl.ds(PAD + start, chunk)],
-            load_sem.at[2 * b + part],
-        ).wait()
-        product = jnp.dot(
-            rows[b, pl.ds(PAD + start, chunk), :], first_weights[...], preferred_element_type=F32
-        )
-        first_products(product, b, pl.ds(LANES + start, chunk), pl.ds(PAD + start, chunk))
-
-    pl.semaphore_wait(barrier, 3 + len(GREETED) + (chips - 1))
+    def first_tile(part):
+        for b in range(batch):
+            loads[2 * b + part].wait()
+        start = part * chunk
+        for b in range(batch):
+            product = jnp.dot(
+                rows[b, PAD + start : PAD + start + chunk, :], first_weights[...],
+                preferred_element_type=F32,
+            )
+            first_products(
+                product, b, slice(LANES + start, LANES + start + chunk),
+                slice(PAD + start, PAD + start + chunk),
+            )
+
+    first_tile(1)
+    pl.semaphore_wait(barrier, 3 + len(GREETED) + 4)
+    greet_round(0)
     halo = remote(
         rows.at[:, pl.ds(PAD + length - HALO, HALO)], rows.at[:, pl.ds(PAD - HALO, HALO)],
         halo_sem.at[0], halo_sem.at[1], seq=after,
@@ -201,6 +213,7 @@
         halo.start()
 
     value_load.start()
+    first_tile(0)
     for load in little[2:]:
         load.wait()
     bias_ref[:, 0:heads] = bias_small[...]
@@ -274,6 +287,8 @@
         ring_own(which, 2)
     for which in range(2):
         ring_own(which, 1)
+
+    greet_round(1)
 
     row = lax.broadcasted_iota(jnp.int32, (BLOCK, BLOCK), 0)
     col = lax.broadcasted_iota(jnp.int32, (BLOCK, BLOCK), 1)
@@ -327,15 +342,14 @@
     convolve(2)
     ring_own(2, 2)
     ring_own(2, 1)
+    greet_round(2)
 
     def gate_part(b, product):
         return silu(product.astype(BF16).astype(F32))
 
     def tile_of(start, size):
         cut = slice(start, start + size)
-
-        @pl.loop(0, batch)
-        def _(b):
+        for b in range(batch):
             if start >= body:
                 product = jnp.dot(
                     rows[b, PAD : PAD + length, :], weights[:, cut], preferred_element_type=F32
@@ -353,6 +367,7 @@
     value_load.wait()
     tile_of(*value_tiles[0])
 
+    greet_round(3)
     pair_log.wait()
     chip_logs[...] = logs[...] + pair_logs[...]
     all_logs[chip] = logs[...] + pair_logs[...]
@@ -361,26 +376,31 @@
             chip_logs, all_logs.at[chip], log_send.at[0], log_recv.at[0],
             seq=2 * chip_at(move) + core,
         ).start()
-    for which in range(2):
-        ring_relay(which, b_way)
-    for start, size in value_tiles[1:]:
-        tile_of(start, size)
-    ring_relay(2, b_way)
-
-    def values_of(g):
+    def values_of(g, low, high):
         b, k = divmod(g, blocks)
         base = PAD + k * BLOCK - HALO
-        wide = jnp.dot(fin[g], expand_ref[...], preferred_element_type=F32)
-        for start in range(0, width, LANES):
+        wide = jnp.dot(fin[g], expand_ref[:, low:high], preferred_element_type=F32)
+        for start in range(low, high, LANES):
             cut = slice(start, start + LANES)
             window = pre[b, base : base + HALO + BLOCK, cut]
             x = conv_ref[0:1, cut] * window
             for tap in range(1, CONV):
                 x = pltpu.roll(x, 1, 0) + conv_ref[tap : tap + 1, cut] * window
-            right[g, STATE:, cut] = (silu(x[HALO:]) * wide[:, cut]).astype(BF16)
-
+            right[g, STATE:, cut] = (
+                silu(x[HALO:]) * wide[:, start - low : start - low + LANES]
+            ).astype(BF16)
+
+    for which in range(2):
+        ring_relay(which, b_way)
     for g in range(total_blocks):
-        values_of(g)
+        values_of(g, 0, TILE)
+        values_of(g, body, width)
+        if g == total_blocks // 2 - 1:
+            ring_relay(2, b_way)
+    for start, size in value_tiles[1:]:
+        tile_of(start, size)
+    for g in range(total_blocks):
+        values_of(g, TILE, body)
     for which in range(3):
         ring_finish(which, 0, b_way)
 
@@ -613,6 +633,7 @@
             pltpu.VMEM((batch, STATE, width), BF16),
             pltpu.VMEM((total_blocks, LANES), F32),
             pltpu.VMEM((tp, total_blocks, LANES), F32),
+            pltpu.SemaphoreType.REGULAR((SIDE // 2 + chips // SIDE // 2 - 1,)),
             dma((2 * batch + 3,)),
             dma((7,)),
             dma((2,)),

time: 41.5 us -> 40.6 us (0.978)
  Pallas kernels: 41.4 us -> 40.3 us
    pallas_call x1, Pallas kernels: 40.2 us -> 39.1 us  [per_device(): pl.pallas_call(mixer_kernel, out_shape=(jax.ShapeDtypeStruct((batch, leng...]
where the time goes in v5:
time: 40.6 us; the launch traced here: 40.5 us
  Pallas kernels  40.3 us (99%)
    pallas_call x1, Pallas kernels, per_device(): pl.pallas_call(mixer_kernel, out_shape=(jax.ShapeDtypeStruct((batch, leng...  39.1 us
    pallas_call x1, Pallas kernels, per_device(): pl.pallas_call(norm_kernel, out_shape=jax.ShapeDtypeStruct((batch, length...  1.22 us

profile of v5, /device:TPU:1, one launch (start us, length us, event | category | flops | bytes accessed | tf_op | source)
XLA Modules:
  0.0 40.5 jit_solution(3369207215948789613)
XLA Ops:
  0.0 39.1 %mixer.1 = (f32[2,512,640]{2,1,0:T(8,128)S(1)}, f32[8,128]{1,0:T(8,128)S(1)}) custom-call(bf16[2,512,2560]{2,1,0:T(8,128)(2,1)} %hidden_ref.1, bf16[2560,640]{1,0:T(8,128)(2,1)} %value_ref.1, bf16[2560,640]{1,0:T(8,128)(2,1)} %gate_ref.1, bf16[32,2560]{1,0:T(8,128)(2,1)} %bitcast.5, bf16[10,2560]{1,0:T(8,128)(2,1)} %bitcast.6, f32[4,640]{1,0:T(4,128)} %conv_in.1, ...), custom_call_target="tpu_custom_call" | custom-call | tf_op jit(solution)/shard_map/mixer/pallas_call | solution.py:585
  39.1 1.2 %norm.1 = bf16[2,512,640]{2,1,0:T(8,128)(2,1)} custom-call(f32[2,512,640]{2,1,0:T(8,128)S(1)} %get-tuple-element.7.gated_ref, f32[8,128]{1,0:T(8,128)S(1)} %get-tuple-element.8.scale_ref), custom_call_target="tpu_custom_call" | custom-call | tf_op jit(solution)/shard_map/norm/pallas_call | solution.py:666

commit v6 on v5

--- a/solution.py
+++ b/solution.py
@@ -164,7 +164,7 @@
 
     for b in range(batch):
         rows[b, 0:HALO, :] = jnp.zeros((HALO, rows.shape[2]), BF16)
-        small_pre[b, 0:LANES, :] = jnp.zeros((LANES, LANES), F32)
+        small_pre[b, 0 : LANES - HALO, :] = jnp.zeros((LANES - HALO, LANES), F32)
     heads = step_cols.shape[0]
     small_ref[0:narrow, :] = jnp.zeros((narrow, small_ref.shape[1]), BF16)
     small_ref[2 * narrow :, :] = jnp.zeros((LANES - 2 * narrow, small_ref.shape[1]), BF16)
@@ -181,39 +181,67 @@
     for at in range(0, small_ref.shape[1], LANES):
         first_weights[at : at + LANES, :LANES] = jnp.transpose(small_ref[:, at : at + LANES])
 
-    def first_products(product, b, small_at, value_at):
-        small_pre[b, small_at, :] = product[:, :LANES]
-        pre[b, value_at, body:] = product[:, LANES:].astype(BF16).astype(F32)
-
     tail_load.wait()
 
     def first_tile(part):
-        for b in range(batch):
-            loads[2 * b + part].wait()
         start = part * chunk
         for b in range(batch):
             product = jnp.dot(
                 rows[b, PAD + start : PAD + start + chunk, :], first_weights[...],
                 preferred_element_type=F32,
             )
-            first_products(
-                product, b, slice(LANES + start, LANES + start + chunk),
-                slice(PAD + start, PAD + start + chunk),
+            small_pre[b, LANES + start : LANES + start + chunk, :] = product[:, :LANES]
+            pre[b, PAD + start : PAD + start + chunk, body:] = (
+                product[:, LANES:].astype(BF16).astype(F32)
             )
 
-    first_tile(1)
-    pl.semaphore_wait(barrier, 3 + len(GREETED) + 4)
-    greet_round(0)
+    for b in range(batch):
+        loads[2 * b + 1].wait()
     halo = remote(
         rows.at[:, pl.ds(PAD + length - HALO, HALO)], rows.at[:, pl.ds(PAD - HALO, HALO)],
         halo_sem.at[0], halo_sem.at[1], seq=after,
     )
-    @pl.when(place < devices - 1)
-    def _():
-        halo.start()
-
+
+    small_halo = remote(
+        small_pre.at[:, pl.ds(LANES + length - HALO, HALO)],
+        small_pre.at[:, pl.ds(LANES - HALO, HALO)],
+        halo_sem.at[2], halo_sem.at[3], seq=after,
+    )
+    tail_halo = remote(
+        pre.at[:, pl.ds(PAD + length - HALO, HALO), pl.ds(body, LANES)],
+        pre.at[:, pl.ds(PAD - HALO, HALO), pl.ds(body, LANES)],
+        halo_sem.at[4], halo_sem.at[5], seq=after,
+    )
+
+    def send_halo(copies, now=True):
+        @pl.when(jnp.logical_and(place < devices - 1, now))
+        def _():
+            for copy in copies:
+                copy.start()
+
+    def wait_halo(copy):
+        @pl.when(place < devices - 1)
+        def _():
+            copy.wait_send()
+
+        @pl.when(place > 0)
+        def _():
+            copy.wait_recv()
+
+    def enter(now, copies):
+        @pl.when(now)
+        def _():
+            pl.semaphore_wait(barrier, 7 + len(GREETED))
+            send_halo(copies)
+
+    enter(me >= ring // 2, [halo])
+    first_tile(1)
+    send_halo([small_halo, tail_halo], me >= ring // 2)
     value_load.start()
+    for b in range(batch):
+        loads[2 * b].wait()
     first_tile(0)
+    enter(me == ring // 2 - 1, [small_halo, tail_halo, halo])
     for load in little[2:]:
         load.wait()
     bias_ref[:, 0:heads] = bias_small[...]
@@ -236,14 +264,14 @@
         bc_wide[b, :, at] = flipped.astype(BF16).astype(F32)
 
     chunks = (
-        (far, far_recv, blocks // 2, blocks, 1),
-        (near, near_recv, 1, blocks // 2, -1),
-        (first_slots, first_recv, 0, 1, -1),
+        (far, far_recv, blocks // 2, blocks),
+        (near, near_recv, 1, blocks // 2),
+        (first_slots, first_recv, 0, 1),
     )
     b_way = jnp.where(jnp.logical_and(me >= 2, me < 2 + ring // 2), 1, -1)
 
     def convolve(which):
-        slots, _, low, high, _ = chunks[which]
+        slots, _, low, high = chunks[which]
         size = (high - low) * BLOCK
         for b in range(batch):
             done = bc_conv(bc_wide[b, :, low * LANES : (high + 1) * LANES])
@@ -263,7 +291,9 @@
         source = tp_at(ring - 2 * way)
         ring_copy(which, source, tp_at(1)).wait_recv()
 
-        @pl.when(way == chunks[which][4])
+        last_way = jnp.where(lax.rem(source, 2) == 0, 1, -1)
+
+        @pl.when(way == last_way)
         def _():
             ring_copy(which, source, tp_at(ring + 2 * way)).start()
 
@@ -284,11 +314,10 @@
             transpose_bc(b, piece)
     for which in range(2):
         convolve(which)
+    enter(me < ring // 2 - 1, [small_halo, tail_halo, halo])
+    greet_round(0)
+    for which in range(2):
         ring_own(which, 2)
-    for which in range(2):
-        ring_own(which, 1)
-
-    greet_round(1)
 
     row = lax.broadcasted_iota(jnp.int32, (BLOCK, BLOCK), 0)
     col = lax.broadcasted_iota(jnp.int32, (BLOCK, BLOCK), 1)
@@ -317,32 +346,22 @@
     pair_log = remote(logs, pair_logs, log_sem.at[0], log_sem.at[1], seq=partner)
     pair_log.start()
 
-    @pl.when(place < devices - 1)
-    def _():
-        halo.wait_send()
-
-    @pl.when(place > 0)
-    def _():
-        halo.wait_recv()
+    wait_halo(small_halo)
 
     @pl.when(place == 0)
     def _():
         for b in range(batch):
             rows[b, 0:PAD, :] = jnp.zeros((PAD, rows.shape[2]), BF16)
-
-    product = jnp.dot(
-        jnp.concatenate([rows[b, 0:PAD, :] for b in range(batch)], axis=0), first_weights[...],
-        preferred_element_type=F32,
-    )
-    for b in range(batch):
-        first_products(
-            product[b * PAD : (b + 1) * PAD], b, slice(LANES - PAD, LANES), slice(0, PAD)
-        )
+            small_pre[b, LANES - HALO : LANES, :] = jnp.zeros((HALO, LANES), F32)
+            pre[b, PAD - HALO : PAD, body:] = jnp.zeros((HALO, LANES), F32)
+
+    for b in range(batch):
         transpose_bc(b, 0)
     convolve(2)
     ring_own(2, 2)
-    ring_own(2, 1)
-    greet_round(2)
+    for which in range(3):
+        ring_own(which, 1)
+    greet_round(1)
 
     def gate_part(b, product):
         return silu(product.astype(BF16).astype(F32))
@@ -365,17 +384,11 @@
     ]
     gate_load.start()
     value_load.wait()
+    wait_halo(halo)
     tile_of(*value_tiles[0])
-
-    greet_round(3)
-    pair_log.wait()
-    chip_logs[...] = logs[...] + pair_logs[...]
-    all_logs[chip] = logs[...] + pair_logs[...]
-    for move in moves:
-        remote(
-            chip_logs, all_logs.at[chip], log_send.at[0], log_recv.at[0],
-            seq=2 * chip_at(move) + core,
-        ).start()
+    wait_halo(tail_halo)
+
+
     def values_of(g, low, high):
         b, k = divmod(g, blocks)
         base = PAD + k * BLOCK - HALO
@@ -392,6 +405,7 @@
 
     for which in range(2):
         ring_relay(which, b_way)
+    greet_round(2)
     for g in range(total_blocks):
         values_of(g, 0, TILE)
         values_of(g, body, width)
@@ -401,11 +415,20 @@
         tile_of(start, size)
     for g in range(total_blocks):
         values_of(g, TILE, body)
+    greet_round(3)
+    pair_log.wait()
+    chip_logs[...] = logs[...] + pair_logs[...]
+    all_logs[chip] = logs[...] + pair_logs[...]
+    for move in moves:
+        remote(
+            chip_logs, all_logs.at[chip], log_send.at[0], log_recv.at[0],
+            seq=2 * chip_at(move) + core,
+        ).start()
     for which in range(3):
         ring_finish(which, 0, b_way)
 
     def bc_block(b, k, first):
-        slots, _, low, high, _ = next(c for c in chunks if c[2] <= k < c[3])
+        slots, _, low, high = next(c for c in chunks if c[2] <= k < c[3])
         at = (b * (high - low) + k - low) * BLOCK
         return slots[first : first + ring // 2, :, at : at + BLOCK].reshape(STATE, BLOCK)
 
@@ -432,20 +455,12 @@
     pair_copy(mine, 2).start()
     for which in range(3):
         ring_relay(which, -b_way)
-    wait_bytes(all_logs, chips - 1, log_send.at[0])
-    wait_bytes(all_logs, chips - 1, log_recv.at[0])
     own_end = jnp.exp(logs[...])
     pair_end = jnp.exp(pair_logs[...])
     wide_ends = jnp.dot(
         halves(jnp.concatenate([own_end, pair_end], axis=0)), expand_ref[...],
         preferred_element_type=F32,
     )
-    low = chip < chips // batch
-    spans = jnp.concatenate(
-        [jnp.where(low, all_logs[i, 0:1, :], all_logs[i, 1:2, :]) for i in range(chips)], axis=0
-    )
-    spans = jnp.dot(halves(jnp.exp(spans)), expand_ref[...], preferred_element_type=F32)
-
     pair_copy(theirs_at, 0).wait()
     groups = chips // batch
     for b in range(batch):
@@ -466,6 +481,13 @@
     for start, size in gate_tiles[:2]:
         tile_of(start, size)
 
+    wait_bytes(all_logs, chips - 1, log_send.at[0])
+    wait_bytes(all_logs, chips - 1, log_recv.at[0])
+    low = chip < chips // batch
+    spans = jnp.concatenate(
+        [jnp.where(low, all_logs[i, 0:1, :], all_logs[i, 1:2, :]) for i in range(chips)], axis=0
+    )
+    spans = jnp.dot(halves(jnp.exp(spans)), expand_ref[...], preferred_element_type=F32)
     wait_bytes(got, chips - 1, out_send.at[0])
     wait_bytes(got, chips - 1, out_recv.at[0])
     running = jnp.zeros((half // groups, width), F32)
@@ -636,7 +658,7 @@
             pltpu.SemaphoreType.REGULAR((SIDE // 2 + chips // SIDE // 2 - 1,)),
             dma((2 * batch + 3,)),
             dma((7,)),
-            dma((2,)),
+            dma((6,)),
             dma((2,)),
             dma((1,)),
             dma((1,)),

time: 40.6 us -> 39.7 us (0.978)
  Pallas kernels: 40.3 us -> 39.4 us
    pallas_call x1, Pallas kernels: 39.1 us -> 38.2 us  [per_device(): pl.pallas_call(mixer_kernel, out_shape=(jax.ShapeDtypeStruct((batch, leng...]
where the time goes in v6:
time: 39.7 us; the launch traced here: 39.6 us
  Pallas kernels  39.4 us (99%)
    pallas_call x1, Pallas kernels, per_device(): pl.pallas_call(mixer_kernel, out_shape=(jax.ShapeDtypeStruct((batch, leng...  38.2 us
    pallas_call x1, Pallas kernels, per_device(): pl.pallas_call(norm_kernel, out_shape=jax.ShapeDtypeStruct((batch, length...  1.22 us

profile of v6, /device:TPU:1, one launch (start us, length us, event | category | flops | bytes accessed | tf_op | source)
XLA Modules:
  0.0 39.6 jit_solution(3436580032211634794)
XLA Ops:
  0.0 38.2 %mixer.1 = (f32[2,512,640]{2,1,0:T(8,128)S(1)}, f32[8,128]{1,0:T(8,128)S(1)}) custom-call(bf16[2,512,2560]{2,1,0:T(8,128)(2,1)} %hidden_ref.1, bf16[2560,640]{1,0:T(8,128)(2,1)} %value_ref.1, bf16[2560,640]{1,0:T(8,128)(2,1)} %gate_ref.1, bf16[32,2560]{1,0:T(8,128)(2,1)} %bitcast.5, bf16[10,2560]{1,0:T(8,128)(2,1)} %bitcast.6, f32[4,640]{1,0:T(4,128)} %conv_in.1, ...), custom_call_target="tpu_custom_call" | custom-call | tf_op jit(solution)/shard_map/mixer/pallas_call | solution.py:607
  38.2 1.2 %norm.1 = bf16[2,512,640]{2,1,0:T(8,128)(2,1)} custom-call(f32[2,512,640]{2,1,0:T(8,128)S(1)} %get-tuple-element.7.gated_ref, f32[8,128]{1,0:T(8,128)S(1)} %get-tuple-element.8.scale_ref), custom_call_target="tpu_custom_call" | custom-call | tf_op jit(solution)/shard_map/norm/pallas_call | solution.py:688

commit v7 on v6

--- a/solution.py
+++ b/solution.py
@@ -291,7 +291,11 @@
         source = tp_at(ring - 2 * way)
         ring_copy(which, source, tp_at(1)).wait_recv()
 
-        last_way = jnp.where(lax.rem(source, 2) == 0, 1, -1)
+        if chunks[which][2] == 0:
+            clockwise = lax.rem(source, ring // 2) < ring // 4
+        else:
+            clockwise = lax.rem(source, 2) == 0
+        last_way = jnp.where(clockwise, 1, -1)
 
         @pl.when(way == last_way)
         def _():
@@ -385,6 +389,7 @@
     gate_load.start()
     value_load.wait()
     wait_halo(halo)
+    ring_relay(0, b_way)
     tile_of(*value_tiles[0])
     wait_halo(tail_halo)
 
@@ -403,14 +408,13 @@
                 silu(x[HALO:]) * wide[:, start - low : start - low + LANES]
             ).astype(BF16)
 
-    for which in range(2):
-        ring_relay(which, b_way)
-    greet_round(2)
+    ring_relay(1, b_way)
     for g in range(total_blocks):
         values_of(g, 0, TILE)
         values_of(g, body, width)
         if g == total_blocks // 2 - 1:
             ring_relay(2, b_way)
+            greet_round(2)
     for start, size in value_tiles[1:]:
         tile_of(start, size)
     for g in range(total_blocks):

time: 39.7 us -> 39.6 us (level)
  no operation moved by 1% of the time
where the time goes in v7:
time: 39.6 us
  Pallas kernels  39.4 us (99%)
    pallas_call x1, Pallas kernels, per_device(): pl.pallas_call(mixer_kernel, out_shape=(jax.ShapeDtypeStruct((batch, leng...  38.2 us
    pallas_call x1, Pallas kernels, per_device(): pl.pallas_call(norm_kernel, out_shape=jax.ShapeDtypeStruct((batch, length...  1.22 us

profile of v7, /device:TPU:1, one launch (start us, length us, event | category | flops | bytes accessed | tf_op | source)
XLA Modules:
  0.0 39.6 jit_solution(14190592977661502606)
XLA Ops:
  0.0 38.2 %mixer.1 = (f32[2,512,640]{2,1,0:T(8,128)S(1)}, f32[8,128]{1,0:T(8,128)S(1)}) custom-call(bf16[2,512,2560]{2,1,0:T(8,128)(2,1)} %hidden_ref.1, bf16[2560,640]{1,0:T(8,128)(2,1)} %value_ref.1, bf16[2560,640]{1,0:T(8,128)(2,1)} %gate_ref.1, bf16[32,2560]{1,0:T(8,128)(2,1)} %bitcast.5, bf16[10,2560]{1,0:T(8,128)(2,1)} %bitcast.6, f32[4,640]{1,0:T(4,128)} %conv_in.1, ...), custom_call_target="tpu_custom_call" | custom-call | tf_op jit(solution)/shard_map/mixer/pallas_call | solution.py:611
  38.2 1.2 %norm.1 = bf16[2,512,640]{2,1,0:T(8,128)(2,1)} custom-call(f32[2,512,640]{2,1,0:T(8,128)S(1)} %get-tuple-element.7.gated_ref, f32[8,128]{1,0:T(8,128)S(1)} %get-tuple-element.8.scale_ref), custom_call_target="tpu_custom_call" | custom-call | tf_op jit(solution)/shard_map/norm/pallas_call | solution.py:692

commit v8 on v6

--- a/solution.py
+++ b/solution.py
@@ -405,12 +405,12 @@
 
     for which in range(2):
         ring_relay(which, b_way)
-    greet_round(2)
     for g in range(total_blocks):
         values_of(g, 0, TILE)
         values_of(g, body, width)
         if g == total_blocks // 2 - 1:
             ring_relay(2, b_way)
+            greet_round(2)
     for start, size in value_tiles[1:]:
         tile_of(start, size)
     for g in range(total_blocks):

time: 39.7 us -> 39.7 us (level)
  no operation moved by 1% of the time
where the time goes in v8:
time: 39.7 us; the launch traced here: 39.6 us
  Pallas kernels  39.4 us (99%)
    pallas_call x1, Pallas kernels, per_device(): pl.pallas_call(mixer_kernel, out_shape=(jax.ShapeDtypeStruct((batch, leng...  38.2 us
    pallas_call x1, Pallas kernels, per_device(): pl.pallas_call(norm_kernel, out_shape=jax.ShapeDtypeStruct((batch, length...  1.22 us

profile of v8, /device:TPU:1, one launch (start us, length us, event | category | flops | bytes accessed | tf_op | source)
XLA Modules:
  0.0 39.6 jit_solution(704841376922838835)
XLA Ops:
  0.0 38.2 %mixer.1 = (f32[2,512,640]{2,1,0:T(8,128)S(1)}, f32[8,128]{1,0:T(8,128)S(1)}) custom-call(bf16[2,512,2560]{2,1,0:T(8,128)(2,1)} %hidden_ref.1, bf16[2560,640]{1,0:T(8,128)(2,1)} %value_ref.1, bf16[2560,640]{1,0:T(8,128)(2,1)} %gate_ref.1, bf16[32,2560]{1,0:T(8,128)(2,1)} %bitcast.5, bf16[10,2560]{1,0:T(8,128)(2,1)} %bitcast.6, f32[4,640]{1,0:T(4,128)} %conv_in.1, ...), custom_call_target="tpu_custom_call" | custom-call | tf_op jit(solution)/shard_map/mixer/pallas_call | solution.py:607
  38.2 1.2 %norm.1 = bf16[2,512,640]{2,1,0:T(8,128)(2,1)} custom-call(f32[2,512,640]{2,1,0:T(8,128)S(1)} %get-tuple-element.7.gated_ref, f32[8,128]{1,0:T(8,128)S(1)} %get-tuple-element.8.scale_ref), custom_call_target="tpu_custom_call" | custom-call | tf_op jit(solution)/shard_map/norm/pallas_call | solution.py:688
